TPU v7x, 16 devices: a 4x2x1 block of a 4x4x8 slice. The times are simulated.
16 devices in a mesh: dp: 2 (over y, z), sp: 8 (over x, core).
Axes of the slice: x: 4, y: 2, z: 1, core: 2. Of those that a mesh axis runs over, the one named last changes fastest.
The devices are a block of a 4x4x8 slice.
Arguments:
- hidden: bfloat16 [32, 128, 2560], P('dp', 'sp'), parts along dimension 0
- attn_norm: bfloat16 [2560], replicated
- w_q: bfloat16 [2560, 32, 128], replicated
- w_k: bfloat16 [2560, 8, 128], replicated
- w_v: bfloat16 [2560, 8, 128], replicated
- w_o: bfloat16 [32, 128, 2560], replicated
- mlp_norm: bfloat16 [2560], replicated
- w_gate: bfloat16 [2560, 9728], replicated
- w_up: bfloat16 [2560, 9728], replicated
- w_down: bfloat16 [9728, 2560], replicated
- mamba_norm: bfloat16 [2560], replicated
- w_in_x: bfloat16 [2560, 5120], replicated
- w_in_z: bfloat16 [2560, 5120], replicated
- conv_w: bfloat16 [4, 5120], replicated
- conv_b: bfloat16 [5120], replicated
- w_xproj: bfloat16 [5120, 192], replicated
- dt_norm: float32 [160], replicated
- b_norm: float32 [16], replicated
- c_norm: float32 [16], replicated
- w_dt: bfloat16 [160, 5120], replicated
- dt_bias: float32 [5120], replicated
- a_log: float32 [5120, 16], replicated
- d_skip: float32 [5120], replicated
- w_out: bfloat16 [5120, 2560], replicated
Outputs:
- output: bfloat16 [32, 128, 2560], P('dp', 'sp'), parts along dimension 0
There are 2 independent parts. A program takes and returns all parts, laid end to end along the dimension named above; an argument that names none is the same for every part.
All inputs are finite; a program needn't handle non-finite values.
Results may differ from a plain program's by a relative error of at most 0.02.
Values are sent between devices in bfloat16 or wider.
A program may use at most 768 MiB of HBM per device.

v0:
```python
import functools
import jax
import jax.numpy as jnp
from jax import lax
from jax.sharding import PartitionSpec as P

EPS = 1e-6
CONV = 4


def rms_scale(values, gain_vec):
    values_f = values.astype(jnp.float32)
    inv_rms = lax.rsqrt(jnp.mean(values_f * values_f, axis=-1, keepdims=True) + EPS)
    return values_f * inv_rms * gain_vec.astype(jnp.float32)


def attention_layer(hidden, attn_norm, w_q, w_k, w_v, w_o):
    n_batch, tok_local, model_dim = hidden.shape
    n_heads, head_dim = w_q.shape[1], w_q.shape[2]
    kv_heads = w_k.shape[1]
    groups = n_heads // kv_heads
    normed = rms_scale(hidden, attn_norm).astype(jnp.bfloat16).reshape(n_batch * tok_local, model_dim)
    queries = jnp.dot(normed, w_q.reshape(model_dim, n_heads * head_dim), preferred_element_type=jnp.float32)
    queries = queries.astype(jnp.bfloat16).reshape(n_batch, tok_local, kv_heads, groups, head_dim)
    key_proj = jnp.dot(normed, w_k.reshape(model_dim, kv_heads * head_dim), preferred_element_type=jnp.float32)
    key_proj = key_proj.astype(jnp.bfloat16).reshape(n_batch, tok_local, kv_heads, head_dim)
    val_proj = jnp.dot(normed, w_v.reshape(model_dim, kv_heads * head_dim), preferred_element_type=jnp.float32)
    val_proj = val_proj.astype(jnp.bfloat16).reshape(n_batch, tok_local, kv_heads, head_dim)
    queries = lax.all_to_all(queries, "sp", 2, 1, tiled=True)
    key_proj = lax.all_to_all(key_proj, "sp", 2, 1, tiled=True)
    val_proj = lax.all_to_all(val_proj, "sp", 2, 1, tiled=True)
    seq_len = key_proj.shape[1]
    causal = lax.broadcasted_iota(jnp.int32, (seq_len, 1), 0) >= lax.broadcasted_iota(jnp.int32, (1, seq_len), 1)
    scores = jnp.einsum("bqngd,bsnd->bngqs", queries, key_proj, preferred_element_type=jnp.float32) * head_dim ** -0.5
    scores = jnp.where(causal, scores, -jnp.inf)
    attn_prob = jax.nn.softmax(scores, axis=-1).astype(jnp.bfloat16)
    attn_out = jnp.einsum("bngqs,bsnd->bqngd", attn_prob, val_proj, preferred_element_type=jnp.float32).astype(jnp.bfloat16)
    attn_out = lax.all_to_all(attn_out, "sp", 1, 2, tiled=True)
    proj_out = jnp.dot(attn_out.reshape(n_batch * tok_local, n_heads * head_dim), w_o.reshape(n_heads * head_dim, model_dim), preferred_element_type=jnp.float32)
    return (hidden.astype(jnp.float32) + proj_out.reshape(n_batch, tok_local, model_dim)).astype(jnp.bfloat16)


def mlp_layer(hidden, mlp_norm, w_gate, w_up, w_down):
    model_dim = hidden.shape[-1]
    normed = rms_scale(hidden, mlp_norm).astype(jnp.bfloat16).reshape(-1, model_dim)
    gate_pre = jnp.dot(normed, w_gate, preferred_element_type=jnp.float32)
    up_proj = jnp.dot(normed, w_up, preferred_element_type=jnp.float32)
    act_val = (jax.nn.silu(gate_pre) * up_proj).astype(jnp.bfloat16)
    down_out = jnp.dot(act_val, w_down, preferred_element_type=jnp.float32)
    return (hidden.astype(jnp.float32) + down_out.reshape(hidden.shape)).astype(jnp.bfloat16)


def mamba_mixer(hidden, mamba_norm, w_in_x, w_in_z, conv_w, conv_b, w_xproj, dt_norm, b_norm, c_norm, w_dt, dt_bias, a_log, d_skip, w_out, n_shards):
    n_batch, tok_local, model_dim = hidden.shape
    n_inner, n_state = a_log.shape
    dt_rank = w_dt.shape[0]
    normed = rms_scale(hidden, mamba_norm).astype(jnp.bfloat16)
    x_inner = jnp.einsum("btd,de->tbe", normed, w_in_x, preferred_element_type=jnp.float32).astype(jnp.bfloat16)
    z_gate = jnp.einsum("btd,de->tbe", normed, w_in_z, preferred_element_type=jnp.float32).astype(jnp.bfloat16)
    shard_idx = lax.axis_index("sp")
    halo_rows = lax.ppermute(x_inner[tok_local - (CONV - 1):], "sp", [(src_idx, src_idx + 1) for src_idx in range(n_shards - 1)])
    padded = jnp.concatenate([halo_rows, x_inner], axis=0)
    conv_acc = conv_b.astype(jnp.float32)
    for tap_idx in range(CONV):
        conv_acc = conv_acc + padded[tap_idx:tap_idx + tok_local].astype(jnp.float32) * conv_w[tap_idx].astype(jnp.float32)
    x_conv = jax.nn.silu(conv_acc).astype(jnp.bfloat16)
    x_dbl = jnp.einsum("tbe,er->tbr", x_conv, w_xproj, preferred_element_type=jnp.float32)
    dt_in = rms_scale(x_dbl[..., :dt_rank], dt_norm).astype(jnp.bfloat16)
    b_mat = rms_scale(x_dbl[..., dt_rank:dt_rank + n_state], b_norm)
    c_mat = rms_scale(x_dbl[..., dt_rank + n_state:], c_norm)
    step_size = jax.nn.softplus(jnp.einsum("tbr,re->tbe", dt_in, w_dt, preferred_element_type=jnp.float32) + dt_bias)
    a_mat = -jnp.exp(a_log)

    def local_step(ssm_state, inputs):
        step_t, x_t, b_t, c_t = inputs
        decay_t = jnp.exp(step_t[:, :, None] * a_mat)
        ssm_state = decay_t * ssm_state + (step_t * x_t.astype(jnp.float32))[:, :, None] * b_t[:, None, :]
        return ssm_state, jnp.sum(ssm_state * c_t[:, None, :], axis=-1)

    def carry_step(ssm_state, inputs):
        step_t, c_t = inputs
        ssm_state = jnp.exp(step_t[:, :, None] * a_mat) * ssm_state
        return ssm_state, jnp.sum(ssm_state * c_t[:, None, :], axis=-1)

    zero_state = jnp.zeros((n_batch, n_inner, n_state), jnp.float32)
    end_state, y_local = lax.scan(local_step, zero_state, (step_size, x_conv, b_mat, c_mat))
    step_total = jnp.sum(step_size, axis=0)
    all_states = lax.all_gather(end_state, "sp")
    all_totals = lax.all_gather(step_total, "sp")
    preceding = jnp.arange(n_shards) < shard_idx
    prec_mask = preceding[:, None, None]
    before_total = jnp.sum(jnp.where(prec_mask, all_totals, 0.0), axis=0)
    gap_sum = jnp.where(prec_mask, before_total[None] - jnp.cumsum(all_totals, axis=0), 0.0)
    carry_weight = jnp.where(preceding[:, None, None, None], jnp.exp(gap_sum[..., None] * a_mat), 0.0)
    start_state = jnp.sum(carry_weight * all_states, axis=0)
    y_carry = lax.scan(carry_step, start_state, (step_size, c_mat))[1]
    y_total = y_local + y_carry + d_skip * x_conv.astype(jnp.float32)
    gated_y = (y_total * jax.nn.silu(z_gate.astype(jnp.float32))).astype(jnp.bfloat16)
    mamba_out = jnp.einsum("tbe,ed->btd", gated_y, w_out, preferred_element_type=jnp.float32)
    return (hidden.astype(jnp.float32) + mamba_out).astype(jnp.bfloat16)


def layer_pair(hidden, attn_norm, w_q, w_k, w_v, w_o, mlp_norm, w_gate, w_up, w_down, mamba_norm, w_in_x, w_in_z, conv_w, conv_b, w_xproj, dt_norm, b_norm, c_norm, w_dt, dt_bias, a_log, d_skip, w_out, n_shards):
    after_attn = attention_layer(hidden, attn_norm, w_q, w_k, w_v, w_o)
    after_mlp = mlp_layer(after_attn, mlp_norm, w_gate, w_up, w_down)
    return mamba_mixer(after_mlp, mamba_norm, w_in_x, w_in_z, conv_w, conv_b, w_xproj, dt_norm, b_norm, c_norm, w_dt, dt_bias, a_log, d_skip, w_out, n_shards)


def solution(mesh):
    act_spec = P("dp", "sp", None)
    return jax.shard_map(
        functools.partial(layer_pair, n_shards=mesh.shape["sp"]),
        mesh=mesh,
        in_specs=(act_spec,) + (P(),) * 23,
        out_specs=act_spec,
        check_vma=False,
    )
```

profile of v0, /device:TPU:112, one launch (start us, length us, event | category | flops | bytes accessed | tf_op | source)
XLA Modules:
  0.0 974.6 jit_solution(12679876995498798616)
XLA Ops:
  35.6 15.9 %fusion.38 = bf16[256,4096]{1,0:T(8,128)(2,1)} fusion(bf16[256,2560]{1,0:T(8,128)(2,1)} %bitcast.216, bf16[320,8,32,128]{3,2,1,0:T(8,128)(2,1)} %bitcast.225), kind=kOutput, calls=%fused_computation.45 | convolution fusion | flops 5369757696 | bytes 24379392 | tf_op jit(solution)/shard_map/dot_general | solution.py:23
  66.9 25.3 %all-to-all-done.2 = bf16[16,16,8,4,128]{4,3,1,0,2:T(4,128)(2,1)} async-done(((bf16[16,16,8,4,128]{4,3,1,0,2:T(4,128)(2,1)}), bf16[16,16,8,4,128]{4,3,1,0,2:T(4,128)(2,1)}, u32[]{:S(2)}, u32[]{:S(2)}) %all-to-all-start.2) | async-done | bytes 2097184 | tf_op jit(solution)/shard_map/all_to_all | solution.py:29
  108.6 26.8 %all-to-all-done.3 = bf16[16,128,1,4,128]{4,3,0,2,1:T(4,128)(2,1)} async-done(((bf16[16,128,1,4,128]{4,3,0,2,1:T(4,128)(2,1)}), bf16[16,128,1,4,128]{4,3,0,2,1:T(4,128)(2,1)}, u32[]{:S(2)}, u32[]{:S(2)}) %all-to-all-start.3) | async-done | bytes 2097184 | tf_op jit(solution)/shard_map/all_to_all | solution.py:38
  146.0 10.8 %fusion.61 = (f32[16,16]{1,0:T(8,128)S(1)}, bf16[16,16,2560]{2,1,0:T(8,128)(2,1)S(1)}) fusion(bf16[16,16,4096]{2,1,0:T(8,128)(2,1)} %dot_general.49, bf16[4096,2560,1]{1,0,2:T(8,128)(2,1)} %bitcast.226, bf16[16,16,2560]{2,1,0:T(8,128)(2,1)} %param.28), kind=kOutput, calls=%fused_computation.71 | convolution fusion | flops 5372641280 | bytes 25691136 | tf_op jit(solution)/shard_map/dot_general | solution.py:39
  159.4 23.8 %fusion.112 = f32[256,9728]{1,0:T(8,128)} fusion(bf16[256,2560]{1,0:T(8,128)(2,1)S(1)} %bitcast.217, bf16[2560,9728]{1,0:T(8,128)(2,1)} %param.35), kind=kOutput, calls=%fused_computation.127 | convolution fusion | flops 12750684160 | bytes 61079552 | tf_op jit(solution)/shard_map/dot_general | solution.py:46
  183.2 24.9 %fusion.10.clone.4 = bf16[256,9728]{1,0:T(8,128)(2,1)} fusion(bf16[256,2560]{1,0:T(8,128)(2,1)} %bitcast.218, bf16[2560,9728]{1,0:T(8,128)(2,1)} %param.36, f32[256,9728]{1,0:T(8,128)} %fusion.112), kind=kOutput, calls=%fused_computation.23.clone.clone.clone.1 | convolution fusion | flops 12765626368 | bytes 66060288 | tf_op jit(solution)/shard_map/dot_general | solution.py:47
  208.2 21.8 %fusion.11 = f32[256,2560]{1,0:T(8,128)S(1)} fusion(bf16[9728,2560]{1,0:T(8,128)(2,1)} %param.37, bf16[256,9728]{1,0:T(8,128)(2,1)} %fusion.10.clone.4), kind=kOutput, calls=%fused_computation.24 | convolution fusion | flops 12750684160 | bytes 57409536 | tf_op jit(solution)/shard_map/dot_general | solution.py:49
  230.5 12.9 %fusion.28 = bf16[16,16,5120]{2,0,1:T(8,128)(2,1)S(1)} fusion(bf16[2560,5120]{1,0:T(8,128)(2,1)} %param.39, bf16[16,16,2560]{2,1,0:T(8,128)(2,1)S(1)} %get-tuple-element.203, f32[2560]{0:T(1024)S(1)} %convert_element_type.174, f32[16,16]{1,0:T(8,128)S(1)} %add_rsqrt_fusion.3), kind=kOutput, calls=%fused_computation.35 | convolution fusion | flops 6714818560 | bytes 30157824 | tf_op jit(solution)/shard_map/btd,de->tbe/dot_general | solution.py:58
  248.8 8.3 multiply_convert_fusion.1
  261.9 8.0 fusion.111
  273.5 224.4 %while.26 = (s32[]{:T(128)}, f32[16,5120,16]{1,2,0:T(8,128)}, f32[16,16,5120]{2,0,1:T(8,128)}, f32[16,16,5120]{2,1,0:T(8,128)}, f32[5120,16]{0,1:T(8,128)S(1)}, ...) while((s32[]{:T(128)}, f32[16,5120,16]{1,2,0:T(8,128)}, ...), condition=%wide.region_10.11_spmd.clone, body=%wide.region_8.10_spmd.clone.sunk | while | flops 9256963 | bytes 14588035 | solution.py:86
  279.7 6.3 dynamic_update_slice.11
  293.8 6.3 dynamic_update_slice.11
  308.0 6.3 dynamic_update_slice.11
  322.1 6.3 dynamic_update_slice.11
  336.2 6.3 dynamic_update_slice.11
  350.4 6.3 dynamic_update_slice.11
  364.5 6.3 dynamic_update_slice.11
  378.6 6.3 dynamic_update_slice.11
  392.8 6.3 dynamic_update_slice.11
  406.9 6.3 dynamic_update_slice.11
  421.0 6.3 dynamic_update_slice.11
  435.1 6.3 dynamic_update_slice.11
  449.2 6.3 dynamic_update_slice.11
  463.3 6.3 dynamic_update_slice.11
  477.4 6.3 dynamic_update_slice.11
  491.6 6.3 dynamic_update_slice.11
  503.5 191.1 %all-gather.7.cloned.1.call-done = f32[128,5120,16]{1,2,0:T(8,128)} async-done(((f32[16,5120,16]{1,2,0:T(8,128)}), f32[128,5120,16]{1,2,0:T(8,128)}) %all-gather.7.cloned.1.call-update) | async-done | bytes 41943056 | tf_op jit(solution)/shard_map/all_gather | solution.py:88
  694.7 17.6 %multiply_reduce_fusion.2 = f32[16,5120,16]{1,2,0:T(8,128)} fusion(f32[8,16,5120,16]{2,3,1,0:T(8,128)} %bitcast.202, f32[5120,16]{0,1:T(8,128)S(1)} %get-tuple-element.368, f32[8,16,5120]{2,1,0:T(8,128)} %fusion.31, pred[8]{0:T(512)(128)(4,1)S(1)} %iota_compare_fusion.1), kind=kLoop, calls=%fused_computation.11 | loop fusion | flops 40632320 | bytes 50135048 | tf_op jit(solution)/shard_map/reduce_sum | solution.py:95
  715.2 220.7 %while.25 = (s32[]{:T(128)}, f32[16,5120,16]{1,2,0:T(8,128)}, f32[16,16,5120]{2,0,1:T(8,128)}, f32[16,16,5120]{2,1,0:T(8,128)}, f32[5120,16]{0,1:T(8,128)S(1)}, ...) while((s32[]{:T(128)}, f32[16,5120,16]{1,2,0:T(8,128)}, f32[16,16,5120]{2,0,1:T(8,128)}, ...), condition=%wide.region_17.18_spmd, body=%wide.region_15.17_spmd.sunk | while | flops 5160962 | bytes 13438049 | solution.py:96
  716.3 6.1 multiply_reduce_fusion.8
  722.7 6.3 dynamic_update_slice.10
  736.5 6.3 dynamic_update_slice.10
  750.3 6.3 dynamic_update_slice.10
  764.1 6.3 dynamic_update_slice.10
  777.9 6.3 dynamic_update_slice.10
  791.7 6.3 dynamic_update_slice.10
  805.5 6.3 dynamic_update_slice.10
  819.2 6.3 dynamic_update_slice.10
  833.0 6.3 dynamic_update_slice.10
  846.8 6.3 dynamic_update_slice.10
  860.6 6.3 dynamic_update_slice.10
  874.4 6.3 dynamic_update_slice.10
  888.2 6.3 dynamic_update_slice.10
  902.0 6.3 dynamic_update_slice.10
  915.8 6.3 dynamic_update_slice.10
  929.6 6.3 dynamic_update_slice.10
  936.0 31.6 %fusion.48 = bf16[16,16,2560]{2,1,0:T(8,128)(2,1)} fusion(bf16[5120,2560]{1,0:T(8,128)(2,1)} %param.51, bf16[16,16,2560]{2,1,0:T(8,128)(2,1)} %copy-done.7, bf16[16,16,5120]{2,0,1:T(8,128)(2,1)} %copy-done.2, f32[16,16,5120]{2,0,1:T(8,128)} %get-tuple-element.80, f32[16,16,5120]{2,0,1:T(8,128)} %get-tuple-element.82, bf16[2560,5120]{1,0:T(8,128)(2,1)} %param.40, ...), kind=kOutput, calls=%fused_computation.64 | convolution fusion | flops 13442088960 | bytes 68189184 | tf_op jit(solution)/shard_map/tbe,ed->btd/dot_general | solution.py:99
  (271 shorter events, 332.2 us)
Async XLA Ops:
  6.5 250.6 %copy-start = (bf16[5120,192]{0,1:T(8,128)(2,1)S(1)}, bf16[5120,192]{0,1:T(8,128)(2,1)}, u32[]{:S(2)}) copy-start(bf16[5120,192]{0,1:T(8,128)(2,1)} %param.43) | copy-start | bytes 5898244
  10.7 4.5 copy-start.8
  16.2 15.6 %all-to-all-start.1 = ((bf16[16,16,8,128]{3,1,0,2:T(8,128)(2,1)}), bf16[16,16,8,128]{3,1,0,2:T(8,128)(2,1)S(1)}, u32[]{:S(2)}, u32[]{:S(2)}) async-start(bf16[16,16,8,128]{3,1,0,2:T(8,128)(2,1)} %copy.97), calls=%async_computation.1 | async-start | bytes 1048576 | tf_op jit(solution)/shard_map/all_to_all | solution.py:30
  31.9 28.2 %all-to-all-start = ((bf16[16,16,8,128]{3,1,0,2:T(8,128)(2,1)}), bf16[16,16,8,128]{3,1,0,2:T(8,128)(2,1)S(1)}, u32[]{:S(2)}, u32[]{:S(2)}) async-start(bf16[16,16,8,128]{3,1,0,2:T(8,128)(2,1)} %copy.95), calls=%async_computation | async-start | bytes 1048576 | tf_op jit(solution)/shard_map/all_to_all | solution.py:31
  60.0 32.2 %all-to-all-start.2 = ((bf16[16,16,8,4,128]{4,3,1,0,2:T(4,128)(2,1)}), bf16[16,16,8,4,128]{4,3,1,0,2:T(4,128)(2,1)}, u32[]{:S(2)}, u32[]{:S(2)}) async-start(bf16[16,16,8,4,128]{4,3,1,0,2:T(4,128)(2,1)} %copy.99), calls=%async_computation.2 | async-start | bytes 4194304 | tf_op jit(solution)/shard_map/all_to_all | solution.py:29
  66.1 28.3 %copy-start.6 = (bf16[16,8,16,1,128]{4,2,1,0,3:T(8,128)(2,1)S(1)}, bf16[16,8,16,1,128]{4,2,1,0,3:T(8,128)(2,1)}, u32[]{:S(2)}) copy-start(bf16[16,8,16,1,128]{4,2,1,0,3:T(8,128)(2,1)} %copy.98) | copy-start | bytes 1572868
  94.4 2.0 copy-start.10
  99.2 9.3 copy-start.14
  99.2 9.3 copy-start.15
  99.2 9.3 copy-start.11
  103.9 31.5 %all-to-all-start.3 = ((bf16[16,128,1,4,128]{4,3,0,2,1:T(4,128)(2,1)}), bf16[16,128,1,4,128]{4,3,0,2,1:T(4,128)(2,1)}, u32[]{:S(2)}, u32[]{:S(2)}) async-start(bf16[16,128,1,4,128]{4,3,0,2,1:T(4,128)(2,1)} %copy.103), calls=%async_computation.3 | async-start | bytes 4194304 | tf_op jit(solution)/shard_map/all_to_all | solution.py:38
  108.4 389.6 %all-gather.5.cloned.1.call-start = ((), (), s32[]{:S(2)}) async-start(), calls=%async_computation.4 | async-start | bytes 2949120 | tf_op jit(solution)/shard_map/all_gather | solution.py:89
  156.9 1.1 copy-start.3
  158.3 1.1 copy-start.9
  208.2 21.8 %copy-start.4 = (bf16[16,16,2560]{2,1,0:T(8,128)(2,1)S(1)}, bf16[16,16,2560]{2,1,0:T(8,128)(2,1)}, u32[]{:S(2)}) copy-start(bf16[16,16,2560]{2,1,0:T(8,128)(2,1)} %copy-done.3) | copy-start | bytes 3932164
  230.4 13.0 %copy-start.7 = (bf16[16,16,2560]{2,1,0:T(8,128)(2,1)}, bf16[16,16,2560]{2,1,0:T(8,128)(2,1)S(1)}, u32[]{:S(2)}) copy-start(bf16[16,16,2560]{2,1,0:T(8,128)(2,1)S(1)} %get-tuple-element.203) | copy-start | bytes 3932164
  230.5 16.4 %copy-start.12 = (bf16[4,5120]{1,0:T(4,128)(2,1)S(1)}, bf16[4,5120]{1,0:T(4,128)(2,1)}, u32[]{:S(2)}) copy-start(bf16[4,5120]{1,0:T(4,128)(2,1)} %param.41) | copy-start | bytes 122884
  230.5 16.5 %copy-start.13 = (bf16[5120]{0:T(1024)(128)(2,1)S(1)}, bf16[5120]{0:T(1024)(128)(2,1)}, u32[]{:S(2)}) copy-start(bf16[5120]{0:T(1024)(128)(2,1)} %param.42) | copy-start | bytes 30724
  243.4 1.5 copy-start.5
  245.5 2.9 collective-permute-start
  257.1 1.5 copy-start.2
  257.1 4.6 copy-start.16
  257.1 4.7 copy-start.19
  261.8 8.4 copy-start.17
  261.9 8.4 copy-start.18
  269.9 424.8 %all-gather.7.cloned.1.call-start = ((), (), s32[]{:S(2)}) async-start(), calls=%async_computation.5 | async-start | bytes 47185920 | tf_op jit(solution)/shard_map/all_gather | solution.py:88
  715.2 220.7 %copy-start.20 = (f32[5120]{0:T(1024)S(1)}, f32[5120]{0:T(1024)}, u32[]{:S(2)}) copy-start(f32[5120]{0:T(1024)} %param.50) | copy-start | bytes 61444
  936.0 31.6 %copy-start.1 = (bf16[5120,192]{0,1:T(8,128)(2,1)S(1)}, bf16[5120,192]{0,1:T(8,128)(2,1)}, u32[]{:S(2)}) copy-start(bf16[5120,192]{0,1:T(8,128)(2,1)} %param.43) | copy-start | bytes 5898244
Sparse Core Ops, SparseCore 0:
  270.0 29.2 all-gather.4
  498.1 196.5 all-gather.6
where the time goes:
time: 989 us; the launch traced here: 975 us
  local copies, waits for them, and re-layouts  289 us (29%)
  waiting for transfers between devices  250 us (25%)
  other arithmetic  237 us (24%)
  matrix products  163 us (16%)
  starting transfers between devices  20.2 us (2%)
  between operations  14.1 us (1%)
    dynamic_update_slice x64, local copies, waits for them, and re-layouts, mamba_mixer(): lax.scan(local_step, zero_state, (step_size, x_conv, b_mat, c_mat))  213 us
    all_gather x1, waiting for transfers between devices, mamba_mixer(): all_states = lax.all_gather(end_state, 'sp')  191 us
    reduce_sum x16, other arithmetic, carry_step(): return (ssm_state, jnp.sum(ssm_state * c_t[:, None, :], axis=-1))  97.8 us
    reduce_sum x16, other arithmetic, local_step(): return (ssm_state, jnp.sum(ssm_state * c_t[:, None, :], axis=-1))  83.4 us
    dot_general x1, matrix products, mamba_mixer(): jnp.einsum('tbe,ed->btd', gated_y, w_out, preferred_element_type=jnp.floa...  31.6 us
    all_to_all x1, waiting for transfers between devices, attention_layer(): attn_out = lax.all_to_all(attn_out, 'sp', 1, 2, tiled=True)  26.8 us
    all_to_all x1, waiting for transfers between devices, attention_layer(): queries = lax.all_to_all(queries, 'sp', 2, 1, tiled=True)  25.3 us
    dot_general x1, matrix products, mlp_layer(): up_proj = jnp.dot(normed, w_up, preferred_element_type=jnp.float32)  24.9 us
  transfers between devices with their start and end apart: 7, of which 5 were waited for; matrix products, arithmetic and copies ran while one was open for 27% of the time, Pallas kernels for 0%

commit v1 on v0

v1 whole, which is shorter than its diff:
```python
import functools
import math

import jax
import jax.numpy as jnp
from jax import lax
from jax.experimental import pallas as pl
from jax.experimental.pallas import tpu as pltpu
from jax.sharding import PartitionSpec as P

EPS = 1e-6
CONV = 4
F32 = jnp.float32
BF16 = jnp.bfloat16
LOG2E = 1.0 / math.log(2.0)


def dot(a, b):
    return jnp.dot(a, b, preferred_element_type=F32)


def dot_nt(a, b):
    return lax.dot_general(a, b, (((1,), (1,)), ((), ())), preferred_element_type=F32)


def rms_rows(v, gain):
    v = v.astype(F32)
    inv = lax.rsqrt(jnp.mean(v * v, axis=-1, keepdims=True) + EPS)
    return v * inv * gain.astype(F32)


def silu(v):
    return v / (1.0 + jnp.exp(-v))


def softplus(v):
    return jnp.maximum(v, 0.0) + jnp.log1p(jnp.exp(-jnp.abs(v)))


def full(shape):
    nd = len(shape)
    return pl.BlockSpec(shape, lambda i: (0,) * nd, pipeline_mode=pl.Buffered(1))


def params(limit=60 << 20):
    return pltpu.CompilerParams(dimension_semantics=("arbitrary",), vmem_limit_bytes=limit)


def attn_kernel(nq, nkv, seq, hd, x_ref, g_ref, wq_ref, wk_ref, wv_ref, wo_ref, h_ref,
                a_s, q_s, kv_s, acc_s):
    i = pl.program_id(0)
    rows, tile = q_s.shape[1], q_s.shape[2]
    grp = tile // hd
    nb = rows // seq
    n1 = nq + 2 * nkv

    @pl.when(i == 0)
    def _():
        a_s[...] = rms_rows(x_ref[...], g_ref[...]).astype(BF16)
        acc_s[...] = x_ref[...].astype(F32)

    @pl.when(i < nq)
    def _():
        q_s[jnp.minimum(i, nq - 1)] = dot(a_s[...], wq_ref[...]).astype(BF16)

    def put_kv(w_ref):
        val = dot(a_s[...], w_ref[...]).astype(BF16)
        base = (i - nq) * grp
        for h in range(grp):
            kv_s[base + h] = val[:, h * hd:(h + 1) * hd]

    @pl.when((i >= nq) & (i < nq + nkv))
    def _():
        put_kv(wk_ref)

    @pl.when((i >= nq + nkv) & (i < n1))
    def _():
        put_kv(wv_ref)

    @pl.when(i >= n1)
    def _():
        j = i - n1
        outs = []
        row_t = lax.broadcasted_iota(jnp.int32, (grp * seq, seq), 0) % seq
        col_t = lax.broadcasted_iota(jnp.int32, (grp * seq, seq), 1)
        causal = row_t >= col_t
        for b in range(nb):
            qb = q_s[j, b * seq:(b + 1) * seq, :]
            q4 = jnp.concatenate([qb[:, g * hd:(g + 1) * hd] for g in range(grp)], axis=0)
            kb = kv_s[j, b * seq:(b + 1) * seq, :]
            vb = kv_s[nkv * grp + j, b * seq:(b + 1) * seq, :]
            s = dot_nt(q4, kb) * (hd ** -0.5)
            s = jnp.where(causal, s, -jnp.inf)
            e = jnp.exp(s - jnp.max(s, axis=-1, keepdims=True))
            p = (e / jnp.sum(e, axis=-1, keepdims=True)).astype(BF16)
            o = dot(p, vb).astype(BF16)
            outs.append(jnp.concatenate([o[g * seq:(g + 1) * seq, :] for g in range(grp)], axis=1))
        o_all = jnp.concatenate(outs, axis=0)
        acc_s[...] += dot(o_all, wo_ref[...])

    @pl.when(i == pl.num_programs(0) - 1)
    def _():
        h_ref[...] = acc_s[...].astype(BF16)


def attention(x, g, wq, wk, wv, wo, seq, hd):
    rows, dm = x.shape
    tile = (wq.shape[1] // wk.shape[1]) * hd
    nq, nkv = wq.shape[1] // tile, wk.shape[1] // tile
    no = wo.shape[0] // tile
    n1 = nq + 2 * nkv
    return pl.pallas_call(
        functools.partial(attn_kernel, nq, nkv, seq, hd),
        grid=(n1 + no,),
        out_shape=jax.ShapeDtypeStruct((rows, dm), BF16),
        in_specs=[
            full((rows, dm)), full((1, dm)),
            pl.BlockSpec((dm, tile), lambda i: (0, jnp.clip(i, 0, nq - 1))),
            pl.BlockSpec((dm, tile), lambda i: (0, jnp.clip(i - nq, 0, nkv - 1))),
            pl.BlockSpec((dm, tile), lambda i: (0, jnp.clip(i - nq - nkv, 0, nkv - 1))),
            pl.BlockSpec((tile, dm), lambda i: (jnp.clip(i - n1, 0, no - 1), 0)),
        ],
        out_specs=full((rows, dm)),
        scratch_shapes=[
            pltpu.VMEM((rows, dm), BF16),
            pltpu.VMEM((nq, rows, tile), BF16),
            pltpu.VMEM((2 * nkv * (tile // hd), rows, hd), BF16),
            pltpu.VMEM((rows, dm), F32),
        ],
        compiler_params=params(),
        name="attention",
    )(x, g, wq, wk, wv, wo)


def mlp_kernel(h_ref, g_ref, wg_ref, wu_ref, wd_ref, o_ref, m_s, act_s, acc_s):
    i = pl.program_id(0)
    n = pl.num_programs(0) - 1

    @pl.when(i == 0)
    def _():
        m_s[...] = rms_rows(h_ref[...], g_ref[...]).astype(BF16)
        acc_s[...] = h_ref[...].astype(F32)
        gate = dot(m_s[...], wg_ref[...])
        up = dot(m_s[...], wu_ref[...])
        act_s[0] = (silu(gate) * up).astype(BF16)

    @pl.when((i > 0) & (i < n))
    def _():
        gate = dot(m_s[...], wg_ref[...])
        up = dot(m_s[...], wu_ref[...])
        acc_s[...] += dot(act_s[lax.rem(i + 1, 2)], wd_ref[...])
        act_s[lax.rem(i, 2)] = (silu(gate) * up).astype(BF16)

    @pl.when(i == n)
    def _():
        o_ref[...] = (acc_s[...] + dot(act_s[lax.rem(i + 1, 2)], wd_ref[...])).astype(BF16)


def mlp(h, g, wg, wu, wd, tile=512):
    rows, dm = h.shape
    n = wg.shape[1] // tile
    return pl.pallas_call(
        mlp_kernel,
        grid=(n + 1,),
        out_shape=jax.ShapeDtypeStruct((rows, dm), BF16),
        in_specs=[
            full((rows, dm)), full((1, dm)),
            pl.BlockSpec((dm, tile), lambda i: (0, jnp.minimum(i, n - 1))),
            pl.BlockSpec((dm, tile), lambda i: (0, jnp.minimum(i, n - 1))),
            pl.BlockSpec((tile, dm), lambda i: (jnp.maximum(i - 1, 0), 0)),
        ],
        out_specs=full((rows, dm)),
        scratch_shapes=[
            pltpu.VMEM((rows, dm), BF16),
            pltpu.VMEM((2, rows, tile), BF16),
            pltpu.VMEM((rows, dm), F32),
        ],
        compiler_params=params(),
        name="mlp",
    )(h, g, wg, wu, wd)


def mamba_kernel(ne, seq, dt_rank, n_state, h_ref, g_ref, wx_ref, cw_ref, cb_ref, wxp_ref,
                 dtn_ref, bn_ref, cn_ref, wdt_ref, dtb_ref, alog_ref, dsk_ref, wz_ref, wo_ref, o_ref,
                 u_s, c_s, r_s, dt_s, b_s, cc_s, d_s, x_s, y_s, a_s, gate_s, acc_s):
    i = pl.program_id(0)
    rows, dm = u_s.shape
    tile = c_s.shape[2]
    sub = tile // 128
    nb = rows // seq

    @pl.when(i == 0)
    def _():
        u_s[...] = rms_rows(h_ref[...], g_ref[...]).astype(BF16)
        acc_s[...] = h_ref[...].astype(F32)
        r_s[...] = jnp.zeros_like(r_s)

    @pl.when(i < ne)
    def _():
        xi = dot(u_s[...], wx_ref[...]).astype(BF16).astype(F32)
        t_idx = lax.broadcasted_iota(jnp.int32, xi.shape, 0) % seq
        acc = cb_ref[...].astype(F32) + xi * cw_ref[CONV - 1:CONV, :].astype(F32)
        for s in range(1, CONV):
            prev = jnp.where(t_idx >= s, pltpu.roll(xi, s, 0), 0.0)
            acc = acc + prev * cw_ref[CONV - 1 - s:CONV - s, :].astype(F32)
        c = silu(acc).astype(BF16)
        c_s[jnp.minimum(i, ne - 1)] = c
        r_s[...] += dot_nt(c, wxp_ref[...])

    @pl.when(i == ne)
    def _():
        r = r_s[...]
        dt_s[...] = rms_rows(r[:, :dt_rank], dtn_ref[...]).astype(BF16)
        bm = rms_rows(r[:, dt_rank:dt_rank + n_state], bn_ref[...])
        cm = rms_rows(r[:, dt_rank + n_state:], cn_ref[...])
        for n in range(n_state):
            b_s[n] = jnp.broadcast_to(bm[:, n:n + 1], (rows, 128))
            cc_s[n] = jnp.broadcast_to(cm[:, n:n + 1], (rows, 128))

    @pl.when(i >= ne)
    def _():
        e = i - ne
        delta = softplus(dot(dt_s[...], wdt_ref[...]) + dtb_ref[...])
        dx = delta * c_s[e].astype(F32)
        a2 = -jnp.exp(alog_ref[...]) * LOG2E
        for j in range(sub):
            d_s[pl.ds(j, rows, stride=sub), :] = delta[:, j * 128:(j + 1) * 128]
            x_s[pl.ds(j, rows, stride=sub), :] = dx[:, j * 128:(j + 1) * 128]
            a_s[pl.ds(j, n_state, stride=sub), :] = a2[:, j * 128:(j + 1) * 128]

        def step(t, state):
            new = []
            for b in range(nb):
                tok = b * seq + t
                row = pl.multiple_of(tok * sub, sub)
                dl = d_s[pl.ds(row, sub), :]
                dxt = x_s[pl.ds(row, sub), :]
                parts = [None] * 4
                for n in range(n_state):
                    bb = b_s[n, pl.ds(tok, sub, stride=0), :]
                    ct = cc_s[n, pl.ds(tok, sub, stride=0), :]
                    s = jnp.exp2(dl * a_s[n * sub:(n + 1) * sub, :]) * state[b * n_state + n] + dxt * bb
                    new.append(s)
                    term = s * ct
                    parts[n % 4] = term if parts[n % 4] is None else parts[n % 4] + term
                y_s[pl.ds(row, sub), :] = (parts[0] + parts[1]) + (parts[2] + parts[3])
            return tuple(new)

        zero = jnp.zeros((sub, 128), F32)
        lax.fori_loop(0, seq, step, (zero,) * (nb * n_state), unroll=2)
        z = dot(u_s[...], wz_ref[...]).astype(BF16).astype(F32)
        for j in range(sub):
            lanes = slice(j * 128, (j + 1) * 128)
            y = y_s[pl.ds(j, rows, stride=sub), :] + dsk_ref[:, lanes] * c_s[e, :, lanes].astype(F32)
            gate_s[:, lanes] = (y * silu(z[:, lanes])).astype(BF16)
        acc_s[...] += dot(gate_s[...], wo_ref[...])

    @pl.when(i == pl.num_programs(0) - 1)
    def _():
        o_ref[...] = acc_s[...].astype(BF16)


def mamba(h, g, wx, wz, cw, cb, wxp_t, dtn, bn, cn, wdt, dtb, alog_t, dsk, wo, seq, tile=1024):
    rows, dm = h.shape
    inner = wx.shape[1]
    dt_rank, n_state = wdt.shape[0], alog_t.shape[0]
    nr = wxp_t.shape[0]
    ne = inner // tile
    sub = tile // 128
    pa = lambda i: (0, jnp.minimum(i, ne - 1))
    pb = lambda i: (0, jnp.maximum(i - ne, 0))
    return pl.pallas_call(
        functools.partial(mamba_kernel, ne, seq, dt_rank, n_state),
        grid=(2 * ne,),
        out_shape=jax.ShapeDtypeStruct((rows, dm), BF16),
        in_specs=[
            full((rows, dm)), full((1, dm)),
            pl.BlockSpec((dm, tile), pa),
            pl.BlockSpec((CONV, tile), pa),
            pl.BlockSpec((1, tile), pa),
            pl.BlockSpec((nr, tile), pa),
            full((1, dt_rank)), full((1, n_state)), full((1, n_state)),
            pl.BlockSpec((dt_rank, tile), pb),
            pl.BlockSpec((1, tile), pb),
            pl.BlockSpec((n_state, tile), pb),
            pl.BlockSpec((1, tile), pb),
            pl.BlockSpec((dm, tile), pb),
            pl.BlockSpec((tile, dm), lambda i: (jnp.maximum(i - ne, 0), 0)),
        ],
        out_specs=full((rows, dm)),
        scratch_shapes=[
            pltpu.VMEM((rows, dm), BF16),
            pltpu.VMEM((ne, rows, tile), BF16),
            pltpu.VMEM((rows, nr), F32),
            pltpu.VMEM((rows, dt_rank), BF16),
            pltpu.VMEM((n_state, rows, 128), F32),
            pltpu.VMEM((n_state, rows, 128), F32),
            pltpu.VMEM((rows * sub, 128), F32),
            pltpu.VMEM((rows * sub, 128), F32),
            pltpu.VMEM((rows * sub, 128), F32),
            pltpu.VMEM((n_state * sub, 128), F32),
            pltpu.VMEM((rows, tile), BF16),
            pltpu.VMEM((rows, dm), F32),
        ],
        compiler_params=params(),
        name="mamba",
    )(h, g, wx, cw, cb, wxp_t, dtn, bn, cn, wdt, dtb, alog_t, dsk, wz, wo)


def layer_pair(hidden, attn_norm, w_q, w_k, w_v, w_o, mlp_norm, w_gate, w_up, w_down, mamba_norm, w_in_x, w_in_z, conv_w, conv_b, w_xproj, dt_norm, b_norm, c_norm, w_dt, dt_bias, a_log, d_skip, w_out):
    dm = hidden.shape[-1]
    hd = w_q.shape[2]
    x = lax.all_to_all(hidden, "sp", 0, 1, tiled=True)
    nb, seq, _ = x.shape
    row = lambda v: v.reshape(1, -1)
    h = x.reshape(nb * seq, dm)
    h = attention(h, row(attn_norm), w_q.reshape(dm, -1), w_k.reshape(dm, -1), w_v.reshape(dm, -1), w_o.reshape(-1, dm), seq, hd)
    h = mlp(h, row(mlp_norm), w_gate, w_up, w_down)
    h = mamba(h, row(mamba_norm), w_in_x, w_in_z, conv_w, row(conv_b), w_xproj.T, row(dt_norm), row(b_norm), row(c_norm), w_dt, row(dt_bias), a_log.T, row(d_skip), w_out, seq)
    return lax.all_to_all(h.reshape(nb, seq, dm), "sp", 1, 0, tiled=True)


def solution(mesh):
    act_spec = P("dp", "sp", None)
    return jax.shard_map(
        layer_pair,
        mesh=mesh,
        in_specs=(act_spec,) + (P(),) * 23,
        out_specs=act_spec,
        check_vma=False,
    )
```

time: 989 us -> 237 us (0.24); the launches traced: 975 us -> 236 us
  waiting for transfers between devices: 250 us -> 0.01 us
  local copies, waits for them, and re-layouts: 289 us -> 40.2 us
  other arithmetic: 237 us -> 0 us
  Pallas kernels: 0 us -> 167 us
  matrix products: 163 us -> 0 us
  blocking collectives: 0 us -> 23.5 us
  starting transfers between devices: 20.2 us -> 5.3 us
  between operations: 14.1 us -> 0.04 us
    dynamic_update_slice x64 -> x0, local copies, waits for them, and re-layouts: 213 us -> none  [mamba_mixer(): lax.scan(local_step, zero_state, (step_size, x_conv, b_mat, c_mat))]
    reduce_sum x39 -> x0, other arithmetic: 205 us -> none  [the longest x16 97.8 us: carry_step(): return (ssm_state, jnp.sum(ssm_state * c_t[:, None, :], axis=-1))]
    all_gather x2 -> x0, waiting for transfers between devices: 191 us -> none  [the longest x1 191 us: mamba_mixer(): all_states = lax.all_gather(end_state, 'sp')]
    pallas_call x0 -> x3, Pallas kernels: none -> 167 us  [the longest x1 71.6 us: mamba(): pl.pallas_call(functools.partial(mamba_kernel, ne, seq, dt_rank, n_state)...]
    dot_general x13 -> x0, matrix products: 163 us -> none  [the longest x1 31.6 us: mamba_mixer(): jnp.einsum('tbe,ed->btd', gated_y, w_out, preferred_element_type=jnp.floa...]
    all_to_all x4 -> x1, waiting for transfers between devices: 57 us -> 0.01 us  [layer_pair(): x = lax.all_to_all(hidden, 'sp', 0, 1, tiled=True)]
    mul x64 -> x0, local copies, waits for them, and re-layouts: 32.3 us -> none  [the longest x16 16 us: local_step(): decay_t = jnp.exp(step_t[:, :, None] * a_mat)]
    all_to_all x0 -> x1, blocking collectives: none -> 23.5 us  [layer_pair(): return lax.all_to_all(h.reshape(nb, seq, dm), 'sp', 1, 0, tiled=True)]
  transfers between devices with their start and end apart: 7 -> 1, of which waited for: 5 -> 0; matrix products, arithmetic and copies ran while one was open for 27% -> 15% of each run, Pallas kernels for 0% -> 0%
where the time goes in v1:
time: 237 us; the launch traced here: 236 us
  Pallas kernels  167 us (70%)
  local copies, waits for them, and re-layouts  40.2 us (17%)
  blocking collectives  23.5 us (10%)
  starting transfers between devices  5.3 us (2%)
    pallas_call x1, Pallas kernels, mamba(): pl.pallas_call(functools.partial(mamba_kernel, ne, seq, dt_rank, n_state)...  71.6 us
    pallas_call x1, Pallas kernels, mlp(): pl.pallas_call(mlp_kernel, grid=(n + 1,), out_shape=jax.ShapeDtypeStruct(...  59.6 us
    pallas_call x1, Pallas kernels, attention(): pl.pallas_call(functools.partial(attn_kernel, nq, nkv, seq, hd), grid=(n1...  36 us
    all_to_all x1, blocking collectives, layer_pair(): return lax.all_to_all(h.reshape(nb, seq, dm), 'sp', 1, 0, tiled=True)  23.5 us
    unnamed x9, local copies, waits for them, and re-layouts  21.3 us
    reshape x1, local copies, waits for them, and re-layouts, layer_pair(): w_v.reshape(dm, -1)  11.4 us
    all_to_all x1, starting transfers between devices, layer_pair(): x = lax.all_to_all(hidden, 'sp', 0, 1, tiled=True)  5.3 us
  transfers between devices with their start and end apart: 1, of which 0 were waited for; matrix products, arithmetic and copies ran while one was open for 15% of the time, Pallas kernels for 0%

profile of v1, /device:TPU:112, one launch (start us, length us, event | category | flops | bytes accessed | tf_op | source)
XLA Modules:
  0.0 236.3 jit_solution(15792933154100298427)
XLA Ops:
  0.0 5.3 %all-to-all-start = ((bf16[16,16,2560]{2,1,0:T(8,128)(2,1)}), bf16[16,16,2560]{2,1,0:T(8,128)(2,1)S(1)}, u32[]{:S(2)}, u32[]{:S(2)}) async-start(bf16[16,16,2560]{2,1,0:T(8,128)(2,1)} %param.24), calls=%async_computation | async-start | bytes 2621440 | tf_op jit(solution)/shard_map/all_to_all | solution.py:313
  5.3 0.0 copy-start.1
  5.3 0.0 copy-start.2
  5.3 0.0 copy-start
  5.3 0.0 copy-start.3
  5.3 21.3 %copy.36 = bf16[320,8,32,128]{3,1,2,0:T(8,128)(2,1)} copy(bf16[320,8,32,128]{3,2,1,0:T(8,128)(2,1)} %bitcast.28) | data formatting | bytes 41943040
  26.7 0.0 copy-done.1
  26.7 0.6 reshape.47.g_ref
  27.3 0.0 copy-done.2
  27.3 0.6 reshape.52.g_ref
  27.9 0.0 copy-done
  27.9 0.6 reshape.54.cb_ref
  28.5 0.0 copy-done.3
  28.5 0.6 reshape.53.g_ref
  29.1 11.4 %copy_bitcast_fusion.1 = (bf16[2560,1024]{1,0:T(8,128)(2,1)}, bf16[2560,1024]{1,0:T(8,128)(2,1)}) fusion(bf16[320,8,8,128]{3,2,1,0:T(8,128)(2,1)} %bitcast.31, bf16[320,8,8,128]{3,2,1,0:T(8,128)(2,1)} %bitcast.32), kind=kLoop, calls=%fused_computation.1 | loop fusion | bytes 20971520 | tf_op jit(solution)/shard_map/reshape | solution.py:317
  40.5 0.0 all-to-all-done
  40.5 1.1 copy.27
  41.7 36.0 %attention.1.h_ref = bf16[256,2560]{1,0:T(8,128)(2,1)} custom-call(bf16[256,2560]{1,0:T(8,128)(2,1)} %bitcast.30, bf16[1,2560]{1,0:T(2,128)(2,1)} %reshape.47.g_ref, bf16[2560,4096]{1,0:T(8,128)(2,1)} %bitcast.27, bf16[2560,1024]{1,0:T(8,128)(2,1)} %get-tuple-element.6.wk_ref, bf16[2560,1024]{1,0:T(8,128)(2,1)} %get-tuple-element.5.wv_ref, ...), custom_call_target="tpu_custom_call" | custom-call | tf_op jit(solution)/shard_map/attention/pallas_call | solution.py:112
  77.7 59.6 %mlp.1.h_ref = bf16[256,2560]{1,0:T(8,128)(2,1)} custom-call(bf16[256,2560]{1,0:T(8,128)(2,1)} %attention.1.h_ref, bf16[1,2560]{1,0:T(2,128)(2,1)} %reshape.52.g_ref, bf16[2560,9728]{1,0:T(8,128)(2,1)} %wg_ref.1, bf16[2560,9728]{1,0:T(8,128)(2,1)} %wu_ref.1, bf16[9728,2560]{1,0:T(8,128)(2,1)} %wd_ref.1), custom_call_target="tpu_custom_call" | custom-call | tf_op jit(solution)/shard_map/mlp/pallas_call | solution.py:162
  137.3 71.6 %mamba.1 = bf16[256,2560]{1,0:T(8,128)(2,1)} custom-call(bf16[256,2560]{1,0:T(8,128)(2,1)} %mlp.1.h_ref, bf16[1,2560]{1,0:T(2,128)(2,1)} %reshape.53.g_ref, bf16[2560,5120]{1,0:T(8,128)(2,1)} %wx_ref.1, bf16[4,5120]{1,0:T(4,128)(2,1)} %cw_ref.1, bf16[1,5120]{1,0:T(2,128)(2,1)} %reshape.54.cb_ref, bf16[192,5120]{1,0:T(8,128)(2,1)} %bitcast.36, ...), custom_call_target="tpu_custom_call" | custom-call | tf_op jit(solution)/shard_map/mamba/pallas_call | solution.py:272
  208.9 2.7 %copy.28 = bf16[2,128,2560]{2,0,1:T(2,128)(2,1)S(1)} copy(bf16[2,128,2560]{2,1,0:T(8,128)(2,1)} %bitcast.35) | data formatting | bytes 2621440 | tf_op jit(solution)/shard_map/reshape | solution.py:320
  211.6 23.5 %all_to_all.33 = bf16[2,128,2560]{2,0,1:T(2,128)(2,1)S(1)} all-to-all(bf16[2,128,2560]{2,0,1:T(2,128)(2,1)S(1)} %copy.28), channel_id=1, replica_groups=mesh['dp'=2,'sp'=8] {'sp'}, dimensions={1} | all-to-all | bytes 2621440 | tf_op jit(solution)/shard_map/all_to_all | solution.py:320
  235.1 1.3 copy.29
Async XLA Ops:
  0.0 40.5 %all-to-all-start = ((bf16[16,16,2560]{2,1,0:T(8,128)(2,1)}), bf16[16,16,2560]{2,1,0:T(8,128)(2,1)S(1)}, u32[]{:S(2)}, u32[]{:S(2)}) async-start(bf16[16,16,2560]{2,1,0:T(8,128)(2,1)} %param.24), calls=%async_computation | async-start | bytes 2621440 | tf_op jit(solution)/shard_map/all_to_all | solution.py:313
  5.3 21.4 %copy-start.1 = (bf16[2560]{0:T(1024)(128)(2,1)S(1)}, bf16[2560]{0:T(1024)(128)(2,1)}, u32[]{:S(2)}) copy-start(bf16[2560]{0:T(1024)(128)(2,1)} %param.25) | copy-start | bytes 15364
  5.3 22.0 %copy-start.2 = (bf16[2560]{0:T(1024)(128)(2,1)S(1)}, bf16[2560]{0:T(1024)(128)(2,1)}, u32[]{:S(2)}) copy-start(bf16[2560]{0:T(1024)(128)(2,1)} %param.30) | copy-start | bytes 15364
  5.3 22.6 %copy-start = (bf16[5120]{0:T(1024)(128)(2,1)S(1)}, bf16[5120]{0:T(1024)(128)(2,1)}, u32[]{:S(2)}) copy-start(bf16[5120]{0:T(1024)(128)(2,1)} %param.38) | copy-start | bytes 30724
  5.3 23.2 %copy-start.3 = (bf16[2560]{0:T(1024)(128)(2,1)S(1)}, bf16[2560]{0:T(1024)(128)(2,1)}, u32[]{:S(2)}) copy-start(bf16[2560]{0:T(1024)(128)(2,1)} %param.34) | copy-start | bytes 15364

commit v2 on v1

v2 whole, which is shorter than its diff:
```python
import functools
import math

import jax
import jax.numpy as jnp
from jax import lax
from jax.experimental import pallas as pl
from jax.experimental.pallas import tpu as pltpu
from jax.sharding import PartitionSpec as P

EPS = 1e-6
CONV = 4
F32 = jnp.float32
BF16 = jnp.bfloat16
MESH = pl.DeviceIdType.MESH
LOG2E = 1.0 / math.log(2.0)


def dot(a, b):
    return jnp.dot(a, b, preferred_element_type=F32)


def dot_nt(a, b):
    return lax.dot_general(a, b, (((1,), (1,)), ((), ())), preferred_element_type=F32)


def rms_rows(v, gain):
    v = v.astype(F32)
    inv = lax.rsqrt(jnp.mean(v * v, axis=-1, keepdims=True) + EPS)
    return v * inv * gain.astype(F32).reshape(1, -1)


def silu(v):
    return v / (1.0 + jnp.exp(-v))


def softplus(v):
    return jnp.maximum(v, 0.0) + jnp.log1p(jnp.exp(-jnp.abs(v)))


def full(shape):
    nd = len(shape)
    return pl.BlockSpec(shape, lambda i: (0,) * nd, pipeline_mode=pl.Buffered(1))


def params(limit=60 << 20):
    return pltpu.CompilerParams(dimension_semantics=("arbitrary",), vmem_limit_bytes=limit)


def ring(n, slots, copies, body):
    for c in range(min(slots, n)):
        for cp in copies(c, c):
            cp.start()

    def run():
        def step(c, _):
            slot = lax.rem(c, slots)
            for cp in copies(c, slot):
                cp.wait()
            body(c, slot)

            @pl.when(c + slots < n)
            def _():
                for cp in copies(c + slots, slot):
                    cp.start()
            return 0
        lax.fori_loop(0, n, step, 0)
    return run


def head_kernel(n, heads, kvh, hd, x_hbm, g_ref, wq_hbm, wk_hbm, wv_hbm, wo_hbm, h_ref,
                x_s, w_s, qb_s, kvb_s, wo_s, a_s, kv_s, q_s, acc_s, pq_s, pk_s,
                ssem, rsem, lsem, qsem, kvsem, osem):
    me = lax.axis_index("sp")
    nb, seq, dm = x_s.shape
    tl = seq // n
    rows = nb * seq
    grp = heads // kvh
    tile = grp * hd
    blk = pq_s.shape[0]
    kq, kk = blk // heads, blk // kvh
    cq, ck = qb_s.shape[1] // heads, kvb_s.shape[2] // kvh

    def q_copies(c, slot):
        m = cq * heads
        return [pltpu.make_async_copy(wq_hbm.at[pl.ds(pl.multiple_of(c * m, m), m)], qb_s.at[slot], qsem.at[slot])]

    def kv_copies(c, slot):
        m = ck * kvh
        return [pltpu.make_async_copy(w.at[pl.ds(pl.multiple_of(c * m, m), m)], kvb_s.at[slot, k], kvsem.at[slot, k])
                for k, w in enumerate((wk_hbm, wv_hbm))]

    def o_copies(c, slot):
        return [pltpu.make_async_copy(wo_hbm.at[pl.ds(pl.multiple_of(c * tile, tile), tile)], wo_s.at[slot], osem.at[slot])]

    def q_body(c, slot):
        def sub(s, _):
            m = 4 * blk
            rhs = jnp.concatenate(
                [qb_s[slot, pl.ds(pl.multiple_of(s * m + i * blk, blk), blk), :] for i in range(4)], axis=1)
            y = dot(pq_s[...], rhs)
            k0 = pl.multiple_of(c * cq + s * 4 * kq, 4 * kq)
            for h in range(heads):
                for p in range(2):
                    pair = [y[h * kq:(h + 1) * kq, (2 * p + e) * hd:(2 * p + e + 1) * hd] for e in range(2)]
                    w_s[pl.ds(k0 + 2 * kq * p, 2 * kq), h * hd:(h + 1) * hd] = jnp.concatenate(pair, axis=0).astype(BF16)
            return 0
        for s in range(cq // (4 * kq)):
            sub(s, 0)

    def kv_body(c, slot):
        def sub(s, _):
            m = 2 * blk
            rhs = jnp.concatenate(
                [kvb_s[slot, k, pl.ds(pl.multiple_of(s * m + i * blk, blk), blk), :] for k in range(2) for i in range(2)], axis=1)
            y = dot(pk_s[...], rhs)
            k0 = pl.multiple_of(c * ck + s * 2 * kk, 2 * kk)
            for k in range(2):
                for i in range(2):
                    for h in range(kvh):
                        col = heads * hd + (k * kvh + h) * hd
                        w_s[pl.ds(k0 + i * kk, kk), col:col + hd] = y[h * kk:(h + 1) * kk, (2 * k + i) * hd:(2 * k + i + 1) * hd].astype(BF16)
            return 0
        for s in range(ck // (2 * kk)):
            sub(s, 0)

    run_kv = ring(dm // ck, kvb_s.shape[0], kv_copies, kv_body)
    run_q = ring(dm // cq, qb_s.shape[0], q_copies, q_body)

    bar = pltpu.get_barrier_semaphore()
    for d in range(1, n):
        pl.semaphore_signal(bar, inc=1, device_id={"sp": lax.rem(me + d, n)}, device_id_type=MESH)
    own = pltpu.make_async_copy(x_hbm.at[pl.ds(me * nb, nb)], x_s.at[:, pl.ds(pl.multiple_of(me * tl, tl), tl), :], lsem)
    own.start()
    r_i = lax.broadcasted_iota(jnp.int32, (blk, blk), 0)
    c_i = lax.broadcasted_iota(jnp.int32, (blk, blk), 1)
    pq_s[...] = jnp.where(c_i == (r_i % kq) * heads + r_i // kq, 1.0, 0.0).astype(BF16)
    pk_s[...] = jnp.where(c_i == (r_i % kk) * kvh + r_i // kk, 1.0, 0.0).astype(BF16)
    pl.semaphore_wait(bar, n - 1)
    sends = []
    half = n // 2
    for d in [half] + [v for k in range(half - 1, 0, -1) for v in (k, n - k)]:
        peer = lax.rem(me + d, n)
        cp = pltpu.make_async_remote_copy(
            src_ref=x_hbm.at[pl.ds(peer * nb, nb)], dst_ref=x_s.at[:, pl.ds(pl.multiple_of(me * tl, tl), tl), :],
            send_sem=ssem.at[d], recv_sem=rsem.at[d], device_id={"sp": peer}, device_id_type=MESH)
        cp.start()
        sends.append(cp)

    run_kv()
    run_q()
    slots_o = wo_s.shape[0]
    n_o = wo_hbm.shape[0] // tile
    for c in range(slots_o):
        for cp in o_copies(c, c):
            cp.start()
    own.wait()
    for cp in sends:
        cp.wait()

    for b in range(nb):
        xb = x_s[b]
        a_s[b * seq:(b + 1) * seq, :] = rms_rows(xb, g_ref[...]).astype(BF16)
        acc_s[b * seq:(b + 1) * seq, :] = xb.astype(F32)

    def kv_proj(c, _):
        col = pl.multiple_of(heads * hd + c * tile, tile)
        val = dot(a_s[...], w_s[:, pl.ds(col, tile)]).astype(BF16)
        for h in range(grp):
            kv_s[c * grp + h] = val[:, h * hd:(h + 1) * hd]
        return 0
    lax.fori_loop(0, 2 * kvh // grp, kv_proj, 0)

    q_s[0] = dot(a_s[...], w_s[:, 0:tile]).astype(BF16)
    row_t = lax.broadcasted_iota(jnp.int32, (grp * seq, seq), 0) % seq
    col_t = lax.broadcasted_iota(jnp.int32, (grp * seq, seq), 1)
    causal = row_t >= col_t

    def group(j, _):
        slot = lax.rem(j, slots_o)
        nxt = jnp.minimum(j + 1, n_o - 1)
        cur = lax.rem(j, 2)
        q_next = dot(a_s[...], w_s[:, pl.ds(pl.multiple_of(nxt * tile, tile), tile)]).astype(BF16)
        outs = []
        for b in range(nb):
            qb = q_s[cur, b * seq:(b + 1) * seq, :]
            q4 = jnp.concatenate([qb[:, g * hd:(g + 1) * hd] for g in range(grp)], axis=0)
            kb = kv_s[j, b * seq:(b + 1) * seq, :]
            vb = kv_s[kvh + j, b * seq:(b + 1) * seq, :]
            s = dot_nt(q4, kb) * (hd ** -0.5)
            s = jnp.where(causal, s, -jnp.inf)
            e = jnp.exp(s - jnp.max(s, axis=-1, keepdims=True))
            p = (e / jnp.sum(e, axis=-1, keepdims=True)).astype(BF16)
            o = dot(p, vb).astype(BF16)
            outs.append(jnp.concatenate([o[g * seq:(g + 1) * seq, :] for g in range(grp)], axis=1))
        q_s[1 - cur] = q_next
        for cp in o_copies(j, slot):
            cp.wait()
        acc_s[...] += dot(jnp.concatenate(outs, axis=0), wo_s[slot])

        @pl.when(j + slots_o < n_o)
        def _():
            for cp in o_copies(j + slots_o, slot):
                cp.start()
        return 0
    lax.fori_loop(0, n_o, group, 0)
    h_ref[...] = acc_s[...].astype(BF16)


def head(x, g, wq, wk, wv, wo, n):
    batch, tl, dm = x.shape
    heads, hd = wq.shape[1:]
    kvh = wk.shape[1]
    nb, seq = batch // n, tl * n
    rows = nb * seq
    grp = heads // kvh
    tile = grp * hd
    blk = 256
    cq, ck, slots_q, slots_o = 128, 320, 3, 3
    any_ = pl.BlockSpec(memory_space=pl.ANY)
    vm = pl.BlockSpec(memory_space=pltpu.VMEM)
    flat = lambda w: w.reshape(-1, w.shape[-1])
    return pl.pallas_call(
        functools.partial(head_kernel, n, heads, kvh, hd),
        out_shape=jax.ShapeDtypeStruct((rows, dm), BF16),
        in_specs=[any_, vm, any_, any_, any_, any_],
        out_specs=vm,
        scratch_shapes=[
            pltpu.VMEM((nb, seq, dm), BF16),
            pltpu.VMEM((dm, (heads + 2 * kvh) * hd), BF16),
            pltpu.VMEM((slots_q, cq * heads, hd), BF16),
            pltpu.VMEM((2, 2, ck * kvh, hd), BF16),
            pltpu.VMEM((slots_o, tile, dm), BF16),
            pltpu.VMEM((rows, dm), BF16),
            pltpu.VMEM((2 * kvh, rows, hd), BF16),
            pltpu.VMEM((2, rows, tile), BF16),
            pltpu.VMEM((rows, dm), F32),
            pltpu.VMEM((blk, blk), BF16),
            pltpu.VMEM((blk, blk), BF16),
            pltpu.SemaphoreType.DMA((n,)),
            pltpu.SemaphoreType.DMA((n,)),
            pltpu.SemaphoreType.DMA,
            pltpu.SemaphoreType.DMA((slots_q,)),
            pltpu.SemaphoreType.DMA((2, 2)),
            pltpu.SemaphoreType.DMA((slots_o,)),
        ],
        compiler_params=pltpu.CompilerParams(collective_id=0, has_side_effects=True, vmem_limit_bytes=63 << 20),
        name="head",
    )(x, g, flat(wq), flat(wk), flat(wv), flat(wo))


def mlp_kernel(h_ref, g_ref, wg_ref, wu_ref, wd_ref, o_ref, m_s, act_s, acc_s):
    i = pl.program_id(0)
    n = pl.num_programs(0) - 1

    @pl.when(i == 0)
    def _():
        m_s[...] = rms_rows(h_ref[...], g_ref[...]).astype(BF16)
        acc_s[...] = h_ref[...].astype(F32)
        gate = dot(m_s[...], wg_ref[...])
        up = dot(m_s[...], wu_ref[...])
        act_s[0] = (silu(gate) * up).astype(BF16)

    @pl.when((i > 0) & (i < n))
    def _():
        gate = dot(m_s[...], wg_ref[...])
        up = dot(m_s[...], wu_ref[...])
        acc_s[...] += dot(act_s[lax.rem(i + 1, 2)], wd_ref[...])
        act_s[lax.rem(i, 2)] = (silu(gate) * up).astype(BF16)

    @pl.when(i == n)
    def _():
        o_ref[...] = (acc_s[...] + dot(act_s[lax.rem(i + 1, 2)], wd_ref[...])).astype(BF16)


def mlp(h, g, wg, wu, wd, tile=512):
    rows, dm = h.shape
    n = wg.shape[1] // tile
    return pl.pallas_call(
        mlp_kernel,
        grid=(n + 1,),
        out_shape=jax.ShapeDtypeStruct((rows, dm), BF16),
        in_specs=[
            full((rows, dm)), full((dm,)),
            pl.BlockSpec((dm, tile), lambda i: (0, jnp.minimum(i, n - 1))),
            pl.BlockSpec((dm, tile), lambda i: (0, jnp.minimum(i, n - 1))),
            pl.BlockSpec((tile, dm), lambda i: (jnp.maximum(i - 1, 0), 0)),
        ],
        out_specs=full((rows, dm)),
        scratch_shapes=[
            pltpu.VMEM((rows, dm), BF16),
            pltpu.VMEM((2, rows, tile), BF16),
            pltpu.VMEM((rows, dm), F32),
        ],
        compiler_params=params(),
        name="mlp",
    )(h, g, wg, wu, wd)


def mamba_kernel(n, ne, seq, dt_rank, n_state, h_ref, g_ref, wx_ref, cw_ref, cb_ref, wxp_ref,
                 dtn_ref, bn_ref, cn_ref, wdt_ref, dtb_ref, alog_ref, dsk_ref, wz_ref, wo_ref, o_hbm,
                 u_s, c_s, r_s, dt_s, b_s, cc_s, d_s, x_s, y_s, a_s, st_s, z_s, gate_s, acc_s, o_s,
                 ssem, rsem, lsem):
    i = pl.program_id(0)
    last = pl.num_programs(0) - 1
    me = lax.axis_index("sp")
    rows, dm = u_s.shape
    tile = c_s.shape[2]
    sub = tile // 128
    nb = rows // seq
    tl = seq // n
    part = 256
    n_part = tile // part
    tc = seq // n_part

    @pl.when(i == 0)
    def _():
        bar = pltpu.get_barrier_semaphore()
        for d in range(1, n):
            pl.semaphore_signal(bar, inc=1, device_id={"sp": lax.rem(me + d, n)}, device_id_type=MESH)
        u_s[...] = rms_rows(h_ref[...], g_ref[...]).astype(BF16)
        acc_s[...] = h_ref[...].astype(F32)
        r_s[...] = jnp.zeros_like(r_s)
        gate_s[...] = jnp.zeros_like(gate_s)

    @pl.when(i < ne)
    def _():
        xi = dot(u_s[...], wx_ref[...]).astype(BF16).astype(F32)
        t_idx = lax.broadcasted_iota(jnp.int32, xi.shape, 0) % seq
        acc = cb_ref[...].astype(F32).reshape(1, -1) + xi * cw_ref[CONV - 1:CONV, :].astype(F32)
        for s in range(1, CONV):
            prev = jnp.where(t_idx >= s, pltpu.roll(xi, s, 0), 0.0)
            acc = acc + prev * cw_ref[CONV - 1 - s:CONV - s, :].astype(F32)
        c = silu(acc).astype(BF16)
        c_s[jnp.minimum(i, ne - 1)] = c
        r_s[...] += dot_nt(c, wxp_ref[...])

    @pl.when(i == ne - 1)
    def _():
        z_s[0] = dot(u_s[...], wz_ref[...]).astype(BF16)
        r = r_s[...]
        dt_s[...] = rms_rows(r[:, :dt_rank], dtn_ref[...]).astype(BF16)
        bm = rms_rows(r[:, dt_rank:dt_rank + n_state], bn_ref[...])
        cm = rms_rows(r[:, dt_rank + n_state:], cn_ref[...])
        for k in range(n_state):
            b_s[k] = jnp.broadcast_to(bm[:, k:k + 1], (rows, 128))
            cc_s[k] = jnp.broadcast_to(cm[:, k:k + 1], (rows, 128))

    @pl.when((i >= ne) & (i < last))
    def _():
        e = i - ne
        zc, zn = lax.rem(e, 2), lax.rem(e + 1, 2)
        delta = softplus(dot(dt_s[...], wdt_ref[...]) + dtb_ref[...])
        dx = delta * c_s[e].astype(F32)
        a2 = -jnp.exp(alog_ref[...]) * LOG2E
        for j in range(sub):
            d_s[pl.ds(j, rows, stride=sub), :] = delta[:, j * 128:(j + 1) * 128]
            x_s[pl.ds(j, rows, stride=sub), :] = dx[:, j * 128:(j + 1) * 128]
            a_s[pl.ds(j, n_state, stride=sub), :] = a2[:, j * 128:(j + 1) * 128]
        st_s[...] = jnp.zeros_like(st_s)

        def chunk(c, _):
            k0 = pl.multiple_of(c * part, part)
            z_s[zn, :, pl.ds(k0, part)] = dot(u_s[...], wz_ref[:, pl.ds(k0, part)]).astype(BF16)
            acc_s[...] += dot(gate_s[:, pl.ds(k0, part)], wo_ref[pl.ds(k0, part), :])
            for b in range(nb):
                state = [st_s[b * n_state + k] for k in range(n_state)]
                for tt in range(tc):
                    tok = b * seq + c * tc + tt
                    row = pl.multiple_of(tok * sub, sub)
                    dl = d_s[pl.ds(row, sub), :]
                    dxt = x_s[pl.ds(row, sub), :]
                    parts = [None] * 2
                    for k in range(n_state):
                        bb = b_s[k, pl.ds(tok, sub, stride=0), :]
                        ct = cc_s[k, pl.ds(tok, sub, stride=0), :]
                        s = jnp.exp2(dl * a_s[k * sub:(k + 1) * sub, :]) * state[k] + dxt * bb
                        state[k] = s
                        term = s * ct
                        parts[k % 2] = term if parts[k % 2] is None else parts[k % 2] + term
                    y_s[pl.ds(row, sub), :] = parts[0] + parts[1]
                for k in range(n_state):
                    st_s[b * n_state + k] = state[k]
            return 0

        lax.fori_loop(0, n_part, chunk, 0)
        for j in range(sub):
            lanes = slice(j * 128, (j + 1) * 128)
            y = y_s[pl.ds(j, rows, stride=sub), :] + dsk_ref[:, lanes] * c_s[e, :, lanes].astype(F32)
            gate_s[:, lanes] = (y * silu(z_s[zc, :, lanes].astype(F32))).astype(BF16)

    @pl.when(i == last)
    def _():
        n_out = o_s.shape[0]
        w = o_s.shape[3]
        pl.semaphore_wait(pltpu.get_barrier_semaphore(), n - 1)
        half = n // 2
        order = [half] + [v for k in range(half - 1, 0, -1) for v in (k, n - k)]
        copies = []

        def send(q):
            lanes = slice(q * w, (q + 1) * w)
            for d in order:
                peer = lax.rem(me + d, n)
                cp = pltpu.make_async_remote_copy(
                    src_ref=o_s.at[q, :, pl.ds(pl.multiple_of(peer * tl, tl), tl), :],
                    dst_ref=o_hbm.at[pl.ds(me * nb, nb), :, lanes],
                    send_sem=ssem.at[q, d], recv_sem=rsem.at[q, d], device_id={"sp": peer}, device_id_type=MESH)
                cp.start()
                copies.append(cp)
            cp = pltpu.make_async_copy(o_s.at[q, :, pl.ds(pl.multiple_of(me * tl, tl), tl), :],
                                       o_hbm.at[pl.ds(me * nb, nb), :, lanes], lsem.at[q])
            cp.start()
            copies.append(cp)

        for q in range(n_out):
            lanes = slice(q * w, (q + 1) * w)
            val = (acc_s[:, lanes] + dot(gate_s[...], wo_ref[:, lanes])).astype(BF16)
            for b in range(nb):
                o_s[q, b] = val[b * seq:(b + 1) * seq, :]
            if q:
                send(q - 1)
        send(n_out - 1)
        for cp in copies:
            cp.wait()


def mamba(h, g, wx, wz, cw, cb, wxp_t, dtn, bn, cn, wdt, dtb, alog_t, dsk, wo, seq, n, tile=1024, n_out=5):
    rows, dm = h.shape
    inner = wx.shape[1]
    dt_rank, n_state = wdt.shape[0], alog_t.shape[0]
    nr = wxp_t.shape[0]
    ne = inner // tile
    sub = tile // 128
    nb, tl = rows // seq, seq // n
    pa = lambda i: (0, jnp.minimum(i, ne - 1))
    pb = lambda i: (0, jnp.clip(i - ne, 0, ne - 1))
    return pl.pallas_call(
        functools.partial(mamba_kernel, n, ne, seq, dt_rank, n_state),
        grid=(2 * ne + 1,),
        out_shape=jax.ShapeDtypeStruct((nb * n, tl, dm), BF16),
        in_specs=[
            full((rows, dm)), full((dm,)),
            pl.BlockSpec((dm, tile), pa),
            pl.BlockSpec((CONV, tile), pa),
            pl.BlockSpec((tile,), lambda i: (jnp.minimum(i, ne - 1),)),
            pl.BlockSpec((nr, tile), pa),
            full((1, dt_rank)), full((1, n_state)), full((1, n_state)),
            pl.BlockSpec((dt_rank, tile), pb),
            pl.BlockSpec((1, tile), pb),
            pl.BlockSpec((n_state, tile), pb),
            pl.BlockSpec((1, tile), pb),
            pl.BlockSpec((dm, tile), lambda i: (0, jnp.clip(i - ne + 1, 0, ne - 1))),
            pl.BlockSpec((tile, dm), lambda i: (jnp.clip(i - ne - 1, 0, ne - 1), 0)),
        ],
        out_specs=pl.BlockSpec(memory_space=pl.ANY),
        scratch_shapes=[
            pltpu.VMEM((rows, dm), BF16),
            pltpu.VMEM((ne, rows, tile), BF16),
            pltpu.VMEM((rows, nr), F32),
            pltpu.VMEM((rows, dt_rank), BF16),
            pltpu.VMEM((n_state, rows, 128), F32),
            pltpu.VMEM((n_state, rows, 128), F32),
            pltpu.VMEM((rows * sub, 128), F32),
            pltpu.VMEM((rows * sub, 128), F32),
            pltpu.VMEM((rows * sub, 128), F32),
            pltpu.VMEM((n_state * sub, 128), F32),
            pltpu.VMEM((nb * n_state, sub, 128), F32),
            pltpu.VMEM((2, rows, tile), BF16),
            pltpu.VMEM((rows, tile), BF16),
            pltpu.VMEM((rows, dm), F32),
            pltpu.VMEM((n_out, nb, seq, dm // n_out), BF16),
            pltpu.SemaphoreType.DMA((n_out, n)),
            pltpu.SemaphoreType.DMA((n_out, n)),
            pltpu.SemaphoreType.DMA((n_out,)),
        ],
        compiler_params=pltpu.CompilerParams(dimension_semantics=("arbitrary",), collective_id=1, has_side_effects=True, vmem_limit_bytes=63 << 20),
        name="mamba",
    )(h, g, wx, cw, cb, wxp_t, dtn, bn, cn, wdt, dtb, alog_t, dsk, wz, wo)


def layer_pair(hidden, attn_norm, w_q, w_k, w_v, w_o, mlp_norm, w_gate, w_up, w_down, mamba_norm, w_in_x, w_in_z, conv_w, conv_b, w_xproj, dt_norm, b_norm, c_norm, w_dt, dt_bias, a_log, d_skip, w_out, n_shards):
    batch, tl, dm = hidden.shape
    seq = tl * n_shards
    row = lambda v: v.reshape(1, -1)
    h = head(hidden, attn_norm, w_q, w_k, w_v, w_o, n_shards)
    h = mlp(h, mlp_norm, w_gate, w_up, w_down)
    return mamba(h, mamba_norm, w_in_x, w_in_z, conv_w, conv_b, w_xproj.T, row(dt_norm), row(b_norm), row(c_norm), w_dt, row(dt_bias), a_log.T, row(d_skip), w_out, seq, n_shards)


def solution(mesh):
    act_spec = P("dp", "sp", None)
    return jax.shard_map(
        functools.partial(layer_pair, n_shards=mesh.shape["sp"]),
        mesh=mesh,
        in_specs=(act_spec,) + (P(),) * 23,
        out_specs=act_spec,
        check_vma=False,
    )
```

time: 237 us -> 192 us (0.81)
  local copies, waits for them, and re-layouts: 40.2 us -> 2.46 us
  blocking collectives: 23.5 us -> 0 us
  Pallas kernels: 167 us -> 189 us
  starting transfers between devices: 5.3 us -> 0 us
    all_to_all x1 -> x0, blocking collectives: 23.5 us -> none  [layer_pair(): return lax.all_to_all(h.reshape(nb, seq, dm), 'sp', 1, 0, tiled=True)]
    pallas_call x2, Pallas kernels: 108 us -> 130 us  [the longest x1 83.6 us: mamba(): pl.pallas_call(functools.partial(mamba_kernel, n, ne, seq, dt_rank, n_sta...]
    unnamed x9 -> x1, local copies, waits for them, and re-layouts: 21.3 us -> 2.46 us
    reshape x6 -> x0, local copies, waits for them, and re-layouts: 16.5 us -> none  [the longest x1 11.4 us: layer_pair(): w_v.reshape(dm, -1)]
    all_to_all x1 -> x0, starting transfers between devices: 5.3 us -> none  [layer_pair(): x = lax.all_to_all(hidden, 'sp', 0, 1, tiled=True)]
    all_to_all x2 -> x0, local copies, waits for them, and re-layouts: 2.4 us -> none  [the longest x1 1.26 us: layer_pair(): return lax.all_to_all(h.reshape(nb, seq, dm), 'sp', 1, 0, tiled=True)]
  transfers between devices with their start and end apart: 1 -> 0, of which waited for: 0 -> 0; matrix products, arithmetic and copies ran while one was open for 15% -> 0% of each run, Pallas kernels for 0% -> 0%
where the time goes in v2:
time: 192 us
  Pallas kernels  189 us (98%)
  local copies, waits for them, and re-layouts  2.46 us (1%)
    pallas_call x1, Pallas kernels, mamba(): pl.pallas_call(functools.partial(mamba_kernel, n, ne, seq, dt_rank, n_sta...  83.6 us
    pallas_call x1, Pallas kernels, mlp(): pl.pallas_call(mlp_kernel, grid=(n + 1,), out_shape=jax.ShapeDtypeStruct(...  59.5 us
    pallas_call x1, Pallas kernels, head(): pl.pallas_call(functools.partial(head_kernel, n, heads, kvh, hd), out_sha...  46.1 us

profile of v2, /device:TPU:112, one launch (start us, length us, event | category | flops | bytes accessed | tf_op | source)
XLA Modules:
  0.0 191.7 jit_solution(3917000846778209944)
XLA Ops:
  0.0 46.1 %head.1.h_ref = bf16[256,2560]{1,0:T(8,128)(2,1)} custom-call(bf16[16,16,2560]{2,1,0:T(8,128)(2,1)} %x_hbm.1, bf16[2560]{0:T(1024)(128)(2,1)} %g_ref.3, bf16[81920,128]{1,0:T(8,128)(2,1)} %bitcast.11, bf16[20480,128]{1,0:T(8,128)(2,1)} %bitcast.13, bf16[20480,128]{1,0:T(8,128)(2,1)} %bitcast.14, bf16[4096,2560]{1,0:T(8,128)(2,1)} %bitcast.12), custom_call_target="tpu_custom_call" | custom-call | tf_op jit(solution)/shard_map/head/pallas_call | solution.py:223
  46.1 59.5 %mlp.1.h_ref = bf16[256,2560]{1,0:T(8,128)(2,1)} custom-call(bf16[256,2560]{1,0:T(8,128)(2,1)} %head.1.h_ref, bf16[2560]{0:T(1024)(128)(2,1)} %g_ref.4, bf16[2560,9728]{1,0:T(8,128)(2,1)} %wg_ref.1, bf16[2560,9728]{1,0:T(8,128)(2,1)} %wu_ref.1, bf16[9728,2560]{1,0:T(8,128)(2,1)} %wd_ref.1), custom_call_target="tpu_custom_call" | custom-call | tf_op jit(solution)/shard_map/mlp/pallas_call | solution.py:279
  105.6 83.6 %mamba.1 = bf16[16,16,2560]{2,1,0:T(8,128)(2,1)} custom-call(bf16[256,2560]{1,0:T(8,128)(2,1)} %mlp.1.h_ref, bf16[2560]{0:T(1024)(128)(2,1)} %g_ref.5, bf16[2560,5120]{1,0:T(8,128)(2,1)} %wx_ref.1, bf16[4,5120]{1,0:T(4,128)(2,1)} %cw_ref.1, bf16[5120]{0:T(1024)(128)(2,1)} %cb_ref.1, bf16[192,5120]{1,0:T(8,128)(2,1)} %bitcast.15, f32[1,160]{1,0:T(1,128)} %bitcast.19, ...), custom_call_target="tpu_custom_call" | custom-call | tf_op jit(solution)/shard_map/mamba/pallas_call | solution.py:438
  189.2 2.5 %copy.26 = bf16[16,16,2560]{2,1,0:T(8,128)(2,1)} copy(bf16[16,16,2560]{2,1,0:T(8,128)(2,1)} %mamba.1) | data formatting | bytes 2621440

commit v3 on v2

--- a/solution.py
+++ b/solution.py
@@ -36,15 +36,6 @@
 
 def softplus(v):
     return jnp.maximum(v, 0.0) + jnp.log1p(jnp.exp(-jnp.abs(v)))
-
-
-def full(shape):
-    nd = len(shape)
-    return pl.BlockSpec(shape, lambda i: (0,) * nd, pipeline_mode=pl.Buffered(1))
-
-
-def params(limit=60 << 20):
-    return pltpu.CompilerParams(dimension_semantics=("arbitrary",), vmem_limit_bytes=limit)
 
 
 def ring(n, slots, copies, body):
@@ -249,127 +240,199 @@
     )(x, g, flat(wq), flat(wk), flat(wv), flat(wo))
 
 
-def mlp_kernel(h_ref, g_ref, wg_ref, wu_ref, wd_ref, o_ref, m_s, act_s, acc_s):
-    i = pl.program_id(0)
-    n = pl.num_programs(0) - 1
-
-    @pl.when(i == 0)
-    def _():
-        m_s[...] = rms_rows(h_ref[...], g_ref[...]).astype(BF16)
-        acc_s[...] = h_ref[...].astype(F32)
-        gate = dot(m_s[...], wg_ref[...])
-        up = dot(m_s[...], wu_ref[...])
-        act_s[0] = (silu(gate) * up).astype(BF16)
-
-    @pl.when((i > 0) & (i < n))
-    def _():
-        gate = dot(m_s[...], wg_ref[...])
-        up = dot(m_s[...], wu_ref[...])
-        acc_s[...] += dot(act_s[lax.rem(i + 1, 2)], wd_ref[...])
-        act_s[lax.rem(i, 2)] = (silu(gate) * up).astype(BF16)
-
-    @pl.when(i == n)
-    def _():
-        o_ref[...] = (acc_s[...] + dot(act_s[lax.rem(i + 1, 2)], wd_ref[...])).astype(BF16)
-
-
-def mlp(h, g, wg, wu, wd, tile=512):
-    rows, dm = h.shape
-    n = wg.shape[1] // tile
-    return pl.pallas_call(
-        mlp_kernel,
-        grid=(n + 1,),
-        out_shape=jax.ShapeDtypeStruct((rows, dm), BF16),
-        in_specs=[
-            full((rows, dm)), full((dm,)),
-            pl.BlockSpec((dm, tile), lambda i: (0, jnp.minimum(i, n - 1))),
-            pl.BlockSpec((dm, tile), lambda i: (0, jnp.minimum(i, n - 1))),
-            pl.BlockSpec((tile, dm), lambda i: (jnp.maximum(i - 1, 0), 0)),
-        ],
-        out_specs=full((rows, dm)),
-        scratch_shapes=[
-            pltpu.VMEM((rows, dm), BF16),
-            pltpu.VMEM((2, rows, tile), BF16),
-            pltpu.VMEM((rows, dm), F32),
-        ],
-        compiler_params=params(),
-        name="mlp",
-    )(h, g, wg, wu, wd)
-
-
-def mamba_kernel(n, ne, seq, dt_rank, n_state, h_ref, g_ref, wx_ref, cw_ref, cb_ref, wxp_ref,
-                 dtn_ref, bn_ref, cn_ref, wdt_ref, dtb_ref, alog_ref, dsk_ref, wz_ref, wo_ref, o_hbm,
-                 u_s, c_s, r_s, dt_s, b_s, cc_s, d_s, x_s, y_s, a_s, st_s, z_s, gate_s, acc_s, o_s,
-                 ssem, rsem, lsem):
-    i = pl.program_id(0)
-    last = pl.num_programs(0) - 1
+def zero_of(vals):
+    return jnp.maximum(functools.reduce(jnp.minimum, vals, jnp.zeros_like(vals[0])), 0.0)
+
+
+def tail_kernel(n, seq, dt_rank, n_state, h_ref, mg_ref, wg_hbm, wu_hbm, wd_hbm, ug_ref, wx_hbm, cw_ref, cb_ref, wxp_hbm,
+                dtn_ref, bn_ref, cn_ref, wdt_hbm, dtb_ref, alog_ref, dsk_ref, wz_hbm, wo_hbm, o_hbm,
+                w_s, d_s, u_s, acc_s, act_s, c_s, xi_s, r_s, dt_s, b_s, cc_s, dl_s, dx_s, y_s, a_s, st_s, z_s, gate_s, o_s,
+                wxp_s, wdt_s, wsem, dsem, psem, ssem, rsem, lsem):
     me = lax.axis_index("sp")
     rows, dm = u_s.shape
-    tile = c_s.shape[2]
+    slots, _, _, half_w = w_s.shape
+    slots_d = d_s.shape[0]
+    tile = 2 * half_w
+    ne, nf = wx_hbm.shape[1] // tile, wg_hbm.shape[1] // half_w
     sub = tile // 128
-    nb = rows // seq
-    tl = seq // n
+    nb, tl = rows // seq, seq // n
     part = 256
     n_part = tile // part
+    per = half_w // part
     tc = seq // n_part
 
-    @pl.when(i == 0)
-    def _():
-        bar = pltpu.get_barrier_semaphore()
-        for d in range(1, n):
-            pl.semaphore_signal(bar, inc=1, device_id={"sp": lax.rem(me + d, n)}, device_id_type=MESH)
-        u_s[...] = rms_rows(h_ref[...], g_ref[...]).astype(BF16)
-        acc_s[...] = h_ref[...].astype(F32)
-        r_s[...] = jnp.zeros_like(r_s)
-        gate_s[...] = jnp.zeros_like(gate_s)
-
-    @pl.when(i < ne)
-    def _():
-        xi = dot(u_s[...], wx_ref[...]).astype(BF16).astype(F32)
+    bar = pltpu.get_barrier_semaphore()
+    for d in range(1, n):
+        pl.semaphore_signal(bar, inc=1, device_id={"sp": lax.rem(me + d, n)}, device_id_type=MESH)
+
+    def w_pair(k, a, b, ka, kb):
+        slot = lax.rem(k, slots)
+        return [pltpu.make_async_copy(w.at[:, pl.ds(pl.multiple_of(q * half_w, half_w), half_w)], w_s.at[slot, r], wsem.at[slot, r])
+                for r, (w, q) in enumerate(((a, ka), (b, kb)))]
+
+    def w_start(k):
+        @pl.when(k < nf)
+        def _():
+            for cp in w_pair(k, wg_hbm, wu_hbm, k, k):
+                cp.start()
+
+        @pl.when((k >= nf) & (k < nf + ne))
+        def _():
+            for cp in w_pair(k, wx_hbm, wx_hbm, 2 * (k - nf), 2 * (k - nf) + 1):
+                cp.start()
+
+        @pl.when((k >= nf + ne) & (k < nf + 2 * ne))
+        def _():
+            for cp in w_pair(k, wz_hbm, wz_hbm, 2 * (k - nf - ne), 2 * (k - nf - ne) + 1):
+                cp.start()
+
+    def w_wait(k):
+        for cp in w_pair(k, wg_hbm, wu_hbm, 0, 0):
+            cp.wait()
+
+    def d_copy(k, w, q):
+        slot = lax.rem(k, slots_d)
+        return pltpu.make_async_copy(w.at[pl.ds(pl.multiple_of(q * half_w, half_w), half_w)], d_s.at[slot], dsem.at[slot])
+
+    def d_start(k):
+        @pl.when(k < nf)
+        def _():
+            d_copy(k, wd_hbm, k).start()
+
+        @pl.when((k >= nf) & (k < nf + 2 * ne))
+        def _():
+            d_copy(k, wo_hbm, k - nf).start()
+
+    def d_wait(k):
+        d_copy(k, wd_hbm, 0).wait()
+
+    for k in range(max(slots, slots_d)):
+        if k < slots:
+            w_start(k)
+        if k < slots_d:
+            d_start(k)
+    small = [pltpu.make_async_copy(wxp_hbm, wxp_s, psem.at[0]), pltpu.make_async_copy(wdt_hbm, wdt_s, psem.at[1])]
+    for cp in small:
+        cp.start()
+
+    u_s[...] = rms_rows(h_ref[...], mg_ref[...]).astype(BF16)
+    acc_s[...] = h_ref[...].astype(F32)
+    w_wait(0)
+    act_s[0] = (silu(dot(u_s[...], w_s[0, 0])) * dot(u_s[...], w_s[0, 1])).astype(BF16)
+    w_start(slots)
+
+    def ff(k, _):
+        slot, prev = lax.rem(k, slots), lax.rem(k - 1, slots_d)
+        w_wait(k)
+        d_wait(k - 1)
+        gate = dot(u_s[...], w_s[slot, 0])
+        up = dot(u_s[...], w_s[slot, 1])
+        acc_s[...] += dot(act_s[lax.rem(k + 1, 2)], d_s[prev])
+        act_s[lax.rem(k, 2)] = (silu(gate) * up).astype(BF16)
+        w_start(k + slots)
+        d_start(k - 1 + slots_d)
+        return 0
+    lax.fori_loop(1, nf, ff, 0)
+    d_wait(nf - 1)
+    h2 = (acc_s[...] + dot(act_s[(nf - 1) % 2], d_s[(nf - 1) % slots_d])).astype(BF16)
+    d_start(nf - 1 + slots_d)
+    acc_s[...] = h2.astype(F32)
+    u_s[...] = rms_rows(acc_s[...], ug_ref[...]).astype(BF16)
+
+    r_s[...] = jnp.zeros_like(r_s)
+    gate_s[...] = jnp.zeros_like(gate_s)
+
+    def in_proj(e):
+        k = nf + e
+        slot = lax.rem(k, slots)
+        w_wait(k)
+        for r in range(2):
+            xi_s[lax.rem(e, 2), :, r * half_w:(r + 1) * half_w] = dot(u_s[...], w_s[slot, r]).astype(BF16)
+
+    def conv(e):
+        col = pl.ds(pl.multiple_of(e * tile, tile), tile)
+        xi = xi_s[lax.rem(e, 2)].astype(F32)
         t_idx = lax.broadcasted_iota(jnp.int32, xi.shape, 0) % seq
-        acc = cb_ref[...].astype(F32).reshape(1, -1) + xi * cw_ref[CONV - 1:CONV, :].astype(F32)
+        acc = cb_ref[col].astype(F32).reshape(1, -1) + xi * cw_ref[CONV - 1:CONV, col].astype(F32)
         for s in range(1, CONV):
             prev = jnp.where(t_idx >= s, pltpu.roll(xi, s, 0), 0.0)
-            acc = acc + prev * cw_ref[CONV - 1 - s:CONV - s, :].astype(F32)
+            acc = acc + prev * cw_ref[CONV - 1 - s:CONV - s, col].astype(F32)
         c = silu(acc).astype(BF16)
-        c_s[jnp.minimum(i, ne - 1)] = c
-        r_s[...] += dot_nt(c, wxp_ref[...])
-
-    @pl.when(i == ne - 1)
-    def _():
-        z_s[0] = dot(u_s[...], wz_ref[...]).astype(BF16)
-        r = r_s[...]
-        dt_s[...] = rms_rows(r[:, :dt_rank], dtn_ref[...]).astype(BF16)
-        bm = rms_rows(r[:, dt_rank:dt_rank + n_state], bn_ref[...])
-        cm = rms_rows(r[:, dt_rank + n_state:], cn_ref[...])
-        for k in range(n_state):
-            b_s[k] = jnp.broadcast_to(bm[:, k:k + 1], (rows, 128))
-            cc_s[k] = jnp.broadcast_to(cm[:, k:k + 1], (rows, 128))
-
-    @pl.when((i >= ne) & (i < last))
-    def _():
-        e = i - ne
+        c_s[e] = c
+        r_s[...] += dot_nt(c, wxp_s[:, col])
+
+    in_proj(0)
+    w_start(nf + slots)
+    for cp in small:
+        cp.wait()
+
+    def phase_a(e, _):
+        in_proj(e)
+        conv(e - 1)
+        w_start(nf + e + slots)
+        return 0
+    lax.fori_loop(1, ne, phase_a, 0)
+
+    kz = nf + ne
+    w_wait(kz)
+    for r in range(2):
+        z_s[0, :, r * half_w:(r + 1) * half_w] = dot(u_s[...], w_s[kz % slots, r]).astype(BF16)
+    conv(ne - 1)
+    w_start(kz + slots)
+
+    r = r_s[...]
+    dt_s[...] = rms_rows(r[:, :dt_rank], dtn_ref[...]).astype(BF16)
+    bm = rms_rows(r[:, dt_rank:dt_rank + n_state], bn_ref[...])
+    cm = rms_rows(r[:, dt_rank + n_state:], cn_ref[...])
+    for k in range(n_state):
+        b_s[k] = jnp.broadcast_to(bm[:, k:k + 1], (rows, 128))
+        cc_s[k] = jnp.broadcast_to(cm[:, k:k + 1], (rows, 128))
+
+    def phase_b(e, _):
+        col = pl.ds(pl.multiple_of(e * tile, tile), tile)
         zc, zn = lax.rem(e, 2), lax.rem(e + 1, 2)
-        delta = softplus(dot(dt_s[...], wdt_ref[...]) + dtb_ref[...])
+        z_tile, o_tile = jnp.minimum(e + 1, ne - 1), jnp.maximum(e - 1, 0)
+        slot_z = lax.rem(kz + z_tile, slots)
+
+        @pl.when(e + 1 < ne)
+        def _():
+            w_wait(kz + e + 1)
+
+        @pl.when(e != 1)
+        def _():
+            for q in range(2):
+                d_wait(nf + 2 * o_tile + q)
+
+        delta = softplus(dot(dt_s[...], wdt_s[:, col]) + dtb_ref[:, col])
         dx = delta * c_s[e].astype(F32)
-        a2 = -jnp.exp(alog_ref[...]) * LOG2E
+        a2 = -jnp.exp(alog_ref[:, col]) * LOG2E
         for j in range(sub):
-            d_s[pl.ds(j, rows, stride=sub), :] = delta[:, j * 128:(j + 1) * 128]
-            x_s[pl.ds(j, rows, stride=sub), :] = dx[:, j * 128:(j + 1) * 128]
+            dl_s[pl.ds(j, rows, stride=sub), :] = delta[:, j * 128:(j + 1) * 128]
+            dx_s[pl.ds(j, rows, stride=sub), :] = dx[:, j * 128:(j + 1) * 128]
             a_s[pl.ds(j, n_state, stride=sub), :] = a2[:, j * 128:(j + 1) * 128]
         st_s[...] = jnp.zeros_like(st_s)
 
         def chunk(c, _):
             k0 = pl.multiple_of(c * part, part)
-            z_s[zn, :, pl.ds(k0, part)] = dot(u_s[...], wz_ref[:, pl.ds(k0, part)]).astype(BF16)
-            acc_s[...] += dot(gate_s[:, pl.ds(k0, part)], wo_ref[pl.ds(k0, part), :])
+            kp = pl.multiple_of(lax.rem(c, per) * part, part)
+            zv = dot(u_s[...], w_s[slot_z, c // per, :, pl.ds(kp, part)])
+            z_s[zn, :, pl.ds(k0, part)] = zv.astype(BF16)
+            slot_o = lax.rem(nf + 2 * o_tile + c // per, slots_d)
+            ov = dot(gate_s[:, pl.ds(k0, part)], d_s[slot_o, pl.ds(kp, part), :])
+            acc_s[...] += ov
+            after_z = zero_of([zv[r0:r0 + 8, l0:l0 + 128] for r0 in (0, rows - 8) for l0 in (0, part - 128)])
+            after_o = zero_of([ov[rows - 8:, l0:l0 + 128] for l0 in range(0, dm, 256)])
             for b in range(nb):
                 state = [st_s[b * n_state + k] for k in range(n_state)]
                 for tt in range(tc):
                     tok = b * seq + c * tc + tt
                     row = pl.multiple_of(tok * sub, sub)
-                    dl = d_s[pl.ds(row, sub), :]
-                    dxt = x_s[pl.ds(row, sub), :]
+                    dl = dl_s[pl.ds(row, sub), :]
+                    dxt = dx_s[pl.ds(row, sub), :]
+                    if b == nb - 1 and tt == 0:
+                        dl = dl + after_z
+                    if b == nb - 1 and tt == tc - 8:
+                        dl = dl + after_o
                     parts = [None] * 2
                     for k in range(n_state):
                         bb = b_s[k, pl.ds(tok, sub, stride=0), :]
@@ -384,79 +447,81 @@
             return 0
 
         lax.fori_loop(0, n_part, chunk, 0)
+        w_start(kz + e + 1 + slots)
+
+        @pl.when(e >= 1)
+        def _():
+            for q in range(2):
+                d_start(nf + 2 * (e - 1) + q + slots_d)
+
         for j in range(sub):
             lanes = slice(j * 128, (j + 1) * 128)
-            y = y_s[pl.ds(j, rows, stride=sub), :] + dsk_ref[:, lanes] * c_s[e, :, lanes].astype(F32)
+            dlanes = pl.ds(pl.multiple_of(e * tile + j * 128, 128), 128)
+            y = y_s[pl.ds(j, rows, stride=sub), :] + dsk_ref[:, dlanes] * c_s[e, :, lanes].astype(F32)
             gate_s[:, lanes] = (y * silu(z_s[zc, :, lanes].astype(F32))).astype(BF16)
-
-    @pl.when(i == last)
-    def _():
-        n_out = o_s.shape[0]
-        w = o_s.shape[3]
-        pl.semaphore_wait(pltpu.get_barrier_semaphore(), n - 1)
-        half = n // 2
-        order = [half] + [v for k in range(half - 1, 0, -1) for v in (k, n - k)]
-        copies = []
-
-        def send(q):
-            lanes = slice(q * w, (q + 1) * w)
-            for d in order:
-                peer = lax.rem(me + d, n)
-                cp = pltpu.make_async_remote_copy(
-                    src_ref=o_s.at[q, :, pl.ds(pl.multiple_of(peer * tl, tl), tl), :],
-                    dst_ref=o_hbm.at[pl.ds(me * nb, nb), :, lanes],
-                    send_sem=ssem.at[q, d], recv_sem=rsem.at[q, d], device_id={"sp": peer}, device_id_type=MESH)
-                cp.start()
-                copies.append(cp)
-            cp = pltpu.make_async_copy(o_s.at[q, :, pl.ds(pl.multiple_of(me * tl, tl), tl), :],
-                                       o_hbm.at[pl.ds(me * nb, nb), :, lanes], lsem.at[q])
+        return 0
+    lax.fori_loop(0, ne, phase_b, 0)
+
+    n_out, _, _, w = o_s.shape
+    pl.semaphore_wait(bar, n - 1)
+    half = n // 2
+    order = [half] + [v for k in range(half - 1, 0, -1) for v in (k, n - k)]
+    copies = []
+
+    def send(q):
+        lanes = slice(q * w, (q + 1) * w)
+        for d in order:
+            peer = lax.rem(me + d, n)
+            cp = pltpu.make_async_remote_copy(
+                src_ref=o_s.at[q, :, pl.ds(pl.multiple_of(peer * tl, tl), tl), :],
+                dst_ref=o_hbm.at[pl.ds(me * nb, nb), :, lanes],
+                send_sem=ssem.at[q, d], recv_sem=rsem.at[q, d], device_id={"sp": peer}, device_id_type=MESH)
             cp.start()
             copies.append(cp)
-
-        for q in range(n_out):
-            lanes = slice(q * w, (q + 1) * w)
-            val = (acc_s[:, lanes] + dot(gate_s[...], wo_ref[:, lanes])).astype(BF16)
-            for b in range(nb):
-                o_s[q, b] = val[b * seq:(b + 1) * seq, :]
-            if q:
-                send(q - 1)
-        send(n_out - 1)
-        for cp in copies:
-            cp.wait()
-
-
-def mamba(h, g, wx, wz, cw, cb, wxp_t, dtn, bn, cn, wdt, dtb, alog_t, dsk, wo, seq, n, tile=1024, n_out=5):
+        cp = pltpu.make_async_copy(o_s.at[q, :, pl.ds(pl.multiple_of(me * tl, tl), tl), :],
+                                   o_hbm.at[pl.ds(me * nb, nb), :, lanes], lsem.at[q])
+        cp.start()
+        copies.append(cp)
+
+    for q in range(2):
+        d_wait(nf + 2 * (ne - 1) + q)
+    s0, s1 = [(nf + 2 * (ne - 1) + q) % slots_d for q in range(2)]
+    for q in range(n_out):
+        lanes = slice(q * w, (q + 1) * w)
+        val = acc_s[:, lanes] + dot(gate_s[:, :half_w], d_s[s0, :, lanes]) + dot(gate_s[:, half_w:], d_s[s1, :, lanes])
+        for b in range(nb):
+            o_s[q, b] = val[b * seq:(b + 1) * seq, :].astype(BF16)
+        if q:
+            send(q - 1)
+    send(n_out - 1)
+    for cp in copies:
+        cp.wait()
+
+
+def tail(h, mg, wg, wu, wd, ug, wx, wz, cw, cb, wxp_t, dtn, bn, cn, wdt, dtb, alog_t, dsk, wo, seq, n, half_w=512, n_out=5, slots=3, slots_d=4):
     rows, dm = h.shape
     inner = wx.shape[1]
     dt_rank, n_state = wdt.shape[0], alog_t.shape[0]
     nr = wxp_t.shape[0]
+    tile = 2 * half_w
     ne = inner // tile
     sub = tile // 128
     nb, tl = rows // seq, seq // n
-    pa = lambda i: (0, jnp.minimum(i, ne - 1))
-    pb = lambda i: (0, jnp.clip(i - ne, 0, ne - 1))
+    any_ = pl.BlockSpec(memory_space=pl.ANY)
+    vm = pl.BlockSpec(memory_space=pltpu.VMEM)
     return pl.pallas_call(
-        functools.partial(mamba_kernel, n, ne, seq, dt_rank, n_state),
-        grid=(2 * ne + 1,),
+        functools.partial(tail_kernel, n, seq, dt_rank, n_state),
         out_shape=jax.ShapeDtypeStruct((nb * n, tl, dm), BF16),
-        in_specs=[
-            full((rows, dm)), full((dm,)),
-            pl.BlockSpec((dm, tile), pa),
-            pl.BlockSpec((CONV, tile), pa),
-            pl.BlockSpec((tile,), lambda i: (jnp.minimum(i, ne - 1),)),
-            pl.BlockSpec((nr, tile), pa),
-            full((1, dt_rank)), full((1, n_state)), full((1, n_state)),
-            pl.BlockSpec((dt_rank, tile), pb),
-            pl.BlockSpec((1, tile), pb),
-            pl.BlockSpec((n_state, tile), pb),
-            pl.BlockSpec((1, tile), pb),
-            pl.BlockSpec((dm, tile), lambda i: (0, jnp.clip(i - ne + 1, 0, ne - 1))),
-            pl.BlockSpec((tile, dm), lambda i: (jnp.clip(i - ne - 1, 0, ne - 1), 0)),
-        ],
-        out_specs=pl.BlockSpec(memory_space=pl.ANY),
+        in_specs=[vm, vm, any_, any_, any_, vm, any_, vm, vm, any_, vm, vm, vm, any_, vm, vm, vm, any_, any_],
+        out_specs=any_,
         scratch_shapes=[
+            pltpu.VMEM((slots, 2, dm, half_w), BF16),
+            pltpu.VMEM((slots_d, half_w, dm), BF16),
             pltpu.VMEM((rows, dm), BF16),
+            pltpu.VMEM((rows, dm), F32),
+            pltpu.VMEM((2, rows, half_w), BF16),
             pltpu.VMEM((ne, rows, tile), BF16),
+            pltpu.VMEM((2, rows, tile), BF16),
             pltpu.VMEM((rows, nr), F32),
             pltpu.VMEM((rows, dt_rank), BF16),
             pltpu.VMEM((n_state, rows, 128), F32),
@@ -468,15 +533,19 @@
             pltpu.VMEM((nb * n_state, sub, 128), F32),
             pltpu.VMEM((2, rows, tile), BF16),
             pltpu.VMEM((rows, tile), BF16),
-            pltpu.VMEM((rows, dm), F32),
             pltpu.VMEM((n_out, nb, seq, dm // n_out), BF16),
+            pltpu.VMEM((nr, inner), BF16),
+            pltpu.VMEM((dt_rank, inner), BF16),
+            pltpu.SemaphoreType.DMA((slots, 2)),
+            pltpu.SemaphoreType.DMA((slots_d,)),
+            pltpu.SemaphoreType.DMA((2,)),
             pltpu.SemaphoreType.DMA((n_out, n)),
             pltpu.SemaphoreType.DMA((n_out, n)),
             pltpu.SemaphoreType.DMA((n_out,)),
         ],
-        compiler_params=pltpu.CompilerParams(dimension_semantics=("arbitrary",), collective_id=1, has_side_effects=True, vmem_limit_bytes=63 << 20),
-        name="mamba",
-    )(h, g, wx, cw, cb, wxp_t, dtn, bn, cn, wdt, dtb, alog_t, dsk, wz, wo)
+        compiler_params=pltpu.CompilerParams(collective_id=1, has_side_effects=True, vmem_limit_bytes=63 << 20),
+        name="tail",
+    )(h, mg, wg, wu, wd, ug, wx, cw, cb, wxp_t, dtn, bn, cn, wdt, dtb, alog_t, dsk, wz, wo)
 
 
 def layer_pair(hidden, attn_norm, w_q, w_k, w_v, w_o, mlp_norm, w_gate, w_up, w_down, mamba_norm, w_in_x, w_in_z, conv_w, conv_b, w_xproj, dt_norm, b_norm, c_norm, w_dt, dt_bias, a_log, d_skip, w_out, n_shards):
@@ -484,8 +553,7 @@
     seq = tl * n_shards
     row = lambda v: v.reshape(1, -1)
     h = head(hidden, attn_norm, w_q, w_k, w_v, w_o, n_shards)
-    h = mlp(h, mlp_norm, w_gate, w_up, w_down)
-    return mamba(h, mamba_norm, w_in_x, w_in_z, conv_w, conv_b, w_xproj.T, row(dt_norm), row(b_norm), row(c_norm), w_dt, row(dt_bias), a_log.T, row(d_skip), w_out, seq, n_shards)
+    return tail(h, mlp_norm, w_gate, w_up, w_down, mamba_norm, w_in_x, w_in_z, conv_w, conv_b, w_xproj.T, row(dt_norm), row(b_norm), row(c_norm), w_dt, row(dt_bias), a_log.T, row(d_skip), w_out, seq, n_shards)
 
 
 def solution(mesh):

time: 192 us -> 175 us (0.911)
  Pallas kernels: 189 us -> 172 us
    pallas_call x2 -> x1, Pallas kernels: 143 us -> 126 us  [tail(): pl.pallas_call(functools.partial(tail_kernel, n, seq, dt_rank, n_state),...]
where the time goes in v3:
time: 175 us; the launch traced here: 174 us
  Pallas kernels  172 us (98%)
  local copies, waits for them, and re-layouts  2.46 us (1%)
    pallas_call x1, Pallas kernels, tail(): pl.pallas_call(functools.partial(tail_kernel, n, seq, dt_rank, n_state),...  126 us
    pallas_call x1, Pallas kernels, head(): pl.pallas_call(functools.partial(head_kernel, n, heads, kvh, hd), out_sha...  46.1 us

profile of v3, /device:TPU:112, one launch (start us, length us, event | category | flops | bytes accessed | tf_op | source)
XLA Modules:
  0.0 174.2 jit_solution(14836520769236538124)
XLA Ops:
  0.0 46.1 %head.1.h_ref = bf16[256,2560]{1,0:T(8,128)(2,1)} custom-call(bf16[16,16,2560]{2,1,0:T(8,128)(2,1)} %x_hbm.1, bf16[2560]{0:T(1024)(128)(2,1)} %g_ref.1, bf16[81920,128]{1,0:T(8,128)(2,1)} %bitcast.11, bf16[20480,128]{1,0:T(8,128)(2,1)} %bitcast.13, bf16[20480,128]{1,0:T(8,128)(2,1)} %bitcast.14, bf16[4096,2560]{1,0:T(8,128)(2,1)} %bitcast.12), custom_call_target="tpu_custom_call" | custom-call | tf_op jit(solution)/shard_map/head/pallas_call | solution.py:214
  46.1 125.6 %tail.1 = bf16[16,16,2560]{2,1,0:T(8,128)(2,1)} custom-call(bf16[256,2560]{1,0:T(8,128)(2,1)} %head.1.h_ref, bf16[2560]{0:T(1024)(128)(2,1)} %mg_ref.1, bf16[2560,9728]{1,0:T(8,128)(2,1)} %wg_hbm.1, bf16[2560,9728]{1,0:T(8,128)(2,1)} %wu_hbm.1, bf16[9728,2560]{1,0:T(8,128)(2,1)} %wd_hbm.1, bf16[2560]{0:T(1024)(128)(2,1)} %ug_ref.1, ...), custom_call_target="tpu_custom_call" | custom-call | tf_op jit(solution)/shard_map/tail/pallas_call | solution.py:512
  171.8 2.5 %copy.26 = bf16[16,16,2560]{2,1,0:T(8,128)(2,1)} copy(bf16[16,16,2560]{2,1,0:T(8,128)(2,1)} %tail.1) | data formatting | bytes 2621440

commit v4 on v3

--- a/solution.py
+++ b/solution.py
@@ -10,6 +10,7 @@
 
 EPS = 1e-6
 CONV = 4
+LAG = 20
 F32 = jnp.float32
 BF16 = jnp.bfloat16
 MESH = pl.DeviceIdType.MESH
@@ -35,7 +36,9 @@
 
 
 def softplus(v):
-    return jnp.maximum(v, 0.0) + jnp.log1p(jnp.exp(-jnp.abs(v)))
+    w = jnp.exp(-jnp.abs(v))
+    u = 1.0 + w
+    return jnp.maximum(v, 0.0) + (jnp.log(u) + (w - (u - 1.0)))
 
 
 def ring(n, slots, copies, body):
@@ -249,7 +252,7 @@
                 w_s, d_s, u_s, acc_s, act_s, c_s, xi_s, r_s, dt_s, b_s, cc_s, dl_s, dx_s, y_s, a_s, st_s, z_s, gate_s, o_s,
                 wxp_s, wdt_s, wsem, dsem, psem, ssem, rsem, lsem):
     me = lax.axis_index("sp")
-    rows, dm = u_s.shape
+    rows, dm = acc_s.shape
     slots, _, _, half_w = w_s.shape
     slots_d = d_s.shape[0]
     tile = 2 * half_w
@@ -315,18 +318,18 @@
     for cp in small:
         cp.start()
 
-    u_s[...] = rms_rows(h_ref[...], mg_ref[...]).astype(BF16)
+    u_s[0:rows, :] = rms_rows(h_ref[...], mg_ref[...]).astype(BF16)
     acc_s[...] = h_ref[...].astype(F32)
     w_wait(0)
-    act_s[0] = (silu(dot(u_s[...], w_s[0, 0])) * dot(u_s[...], w_s[0, 1])).astype(BF16)
+    act_s[0] = (silu(dot(u_s[0:rows, :], w_s[0, 0])) * dot(u_s[0:rows, :], w_s[0, 1])).astype(BF16)
     w_start(slots)
 
     def ff(k, _):
         slot, prev = lax.rem(k, slots), lax.rem(k - 1, slots_d)
         w_wait(k)
         d_wait(k - 1)
-        gate = dot(u_s[...], w_s[slot, 0])
-        up = dot(u_s[...], w_s[slot, 1])
+        gate = dot(u_s[0:rows, :], w_s[slot, 0])
+        up = dot(u_s[0:rows, :], w_s[slot, 1])
         acc_s[...] += dot(act_s[lax.rem(k + 1, 2)], d_s[prev])
         act_s[lax.rem(k, 2)] = (silu(gate) * up).astype(BF16)
         w_start(k + slots)
@@ -337,7 +340,7 @@
     h2 = (acc_s[...] + dot(act_s[(nf - 1) % 2], d_s[(nf - 1) % slots_d])).astype(BF16)
     d_start(nf - 1 + slots_d)
     acc_s[...] = h2.astype(F32)
-    u_s[...] = rms_rows(acc_s[...], ug_ref[...]).astype(BF16)
+    u_s[0:rows, :] = rms_rows(acc_s[...], ug_ref[...]).astype(BF16)
 
     r_s[...] = jnp.zeros_like(r_s)
     gate_s[...] = jnp.zeros_like(gate_s)
@@ -347,7 +350,7 @@
         slot = lax.rem(k, slots)
         w_wait(k)
         for r in range(2):
-            xi_s[lax.rem(e, 2), :, r * half_w:(r + 1) * half_w] = dot(u_s[...], w_s[slot, r]).astype(BF16)
+            xi_s[lax.rem(e, 2), :, r * half_w:(r + 1) * half_w] = dot(u_s[0:rows, :], w_s[slot, r]).astype(BF16)
 
     def conv(e):
         col = pl.ds(pl.multiple_of(e * tile, tile), tile)
@@ -376,7 +379,7 @@
     kz = nf + ne
     w_wait(kz)
     for r in range(2):
-        z_s[0, :, r * half_w:(r + 1) * half_w] = dot(u_s[...], w_s[kz % slots, r]).astype(BF16)
+        z_s[0, :, r * half_w:(r + 1) * half_w] = dot(u_s[0:rows, :], w_s[kz % slots, r]).astype(BF16)
     conv(ne - 1)
     w_start(kz + slots)
 
@@ -413,26 +416,27 @@
         st_s[...] = jnp.zeros_like(st_s)
 
         def chunk(c, _):
+            spare = pl.multiple_of(rows + 16 * lax.div(c, n_part), 16)
             k0 = pl.multiple_of(c * part, part)
             kp = pl.multiple_of(lax.rem(c, per) * part, part)
-            zv = dot(u_s[...], w_s[slot_z, c // per, :, pl.ds(kp, part)])
-            z_s[zn, :, pl.ds(k0, part)] = zv.astype(BF16)
             slot_o = lax.rem(nf + 2 * o_tile + c // per, slots_d)
-            ov = dot(gate_s[:, pl.ds(k0, part)], d_s[slot_o, pl.ds(kp, part), :])
-            acc_s[...] += ov
-            after_z = zero_of([zv[r0:r0 + 8, l0:l0 + 128] for r0 in (0, rows - 8) for l0 in (0, part - 128)])
-            after_o = zero_of([ov[rows - 8:, l0:l0 + 128] for l0 in range(0, dm, 256)])
+            n_k = dm // 256
+            places = [(p * (nb * tc - LAG)) // (2 * n_k) for p in range(2 * n_k)]
+            lhs, after = [], {}
+
+            def fence(ref, y):
+                ref[pl.ds(spare, 16), 0:128] = jnp.concatenate([y, y], axis=0).astype(BF16)
+
             for b in range(nb):
                 state = [st_s[b * n_state + k] for k in range(n_state)]
                 for tt in range(tc):
+                    step = b * tc + tt
                     tok = b * seq + c * tc + tt
                     row = pl.multiple_of(tok * sub, sub)
                     dl = dl_s[pl.ds(row, sub), :]
                     dxt = dx_s[pl.ds(row, sub), :]
-                    if b == nb - 1 and tt == 0:
-                        dl = dl + after_z
-                    if b == nb - 1 and tt == tc - 8:
-                        dl = dl + after_o
+                    if step in after:
+                        dl = dl + after[step]
                     parts = [None] * 2
                     for k in range(n_state):
                         bb = b_s[k, pl.ds(tok, sub, stride=0), :]
@@ -441,7 +445,26 @@
                         state[k] = s
                         term = s * ct
                         parts[k % 2] = term if parts[k % 2] is None else parts[k % 2] + term
-                    y_s[pl.ds(row, sub), :] = parts[0] + parts[1]
+                    y = parts[0] + parts[1]
+                    y_s[pl.ds(row, sub), :] = y
+                    if step == tc - 1:
+                        after[tc] = zero_of([y])
+                    if step in places:
+                        p = places.index(step)
+                        q = p // 2
+                        if p % 2 == 0:
+                            fence(u_s, y)
+                            lhs.append(u_s[0:rows, q * 256:(q + 1) * 256])
+                        else:
+                            fence(gate_s, y)
+                            lanes = slice(q * 256, (q + 1) * 256)
+                            ov = dot(gate_s[0:rows, pl.ds(k0, part)], d_s[slot_o, pl.ds(kp, part), lanes])
+                            acc_s[:, lanes] += ov
+                            after[step + LAG] = zero_of([ov[rows - 8:, l0:l0 + 128] for l0 in (0, 128)])
+                        if p == 2 * n_k - 2:
+                            zv = dot(jnp.concatenate(lhs, axis=1), w_s[slot_z, c // per, :, pl.ds(kp, part)])
+                            z_s[zn, :, pl.ds(k0, part)] = zv.astype(BF16)
+                            after[step + LAG] = zero_of([zv[r0:r0 + 8, l0:l0 + 128] for r0 in (0, rows - 8) for l0 in (0, part - 128)])
                 for k in range(n_state):
                     st_s[b * n_state + k] = state[k]
             return 0
@@ -458,7 +481,7 @@
             lanes = slice(j * 128, (j + 1) * 128)
             dlanes = pl.ds(pl.multiple_of(e * tile + j * 128, 128), 128)
             y = y_s[pl.ds(j, rows, stride=sub), :] + dsk_ref[:, dlanes] * c_s[e, :, lanes].astype(F32)
-            gate_s[:, lanes] = (y * silu(z_s[zc, :, lanes].astype(F32))).astype(BF16)
+            gate_s[0:rows, lanes] = (y * silu(z_s[zc, :, lanes].astype(F32))).astype(BF16)
         return 0
     lax.fori_loop(0, ne, phase_b, 0)
 
@@ -488,7 +511,7 @@
     s0, s1 = [(nf + 2 * (ne - 1) + q) % slots_d for q in range(2)]
     for q in range(n_out):
         lanes = slice(q * w, (q + 1) * w)
-        val = acc_s[:, lanes] + dot(gate_s[:, :half_w], d_s[s0, :, lanes]) + dot(gate_s[:, half_w:], d_s[s1, :, lanes])
+        val = acc_s[:, lanes] + dot(gate_s[0:rows, :half_w], d_s[s0, :, lanes]) + dot(gate_s[0:rows, half_w:], d_s[s1, :, lanes])
         for b in range(nb):
             o_s[q, b] = val[b * seq:(b + 1) * seq, :].astype(BF16)
         if q:
@@ -517,7 +540,7 @@
         scratch_shapes=[
             pltpu.VMEM((slots, 2, dm, half_w), BF16),
             pltpu.VMEM((slots_d, half_w, dm), BF16),
-            pltpu.VMEM((rows, dm), BF16),
+            pltpu.VMEM((rows + 16, dm), BF16),
             pltpu.VMEM((rows, dm), F32),
             pltpu.VMEM((2, rows, half_w), BF16),
             pltpu.VMEM((ne, rows, tile), BF16),
@@ -532,7 +555,7 @@
             pltpu.VMEM((n_state * sub, 128), F32),
             pltpu.VMEM((nb * n_state, sub, 128), F32),
             pltpu.VMEM((2, rows, tile), BF16),
-            pltpu.VMEM((rows, tile), BF16),
+            pltpu.VMEM((rows + 16, tile), BF16),
             pltpu.VMEM((n_out, nb, seq, dm // n_out), BF16),
             pltpu.VMEM((nr, inner), BF16),
             pltpu.VMEM((dt_rank, inner), BF16),
@@ -543,7 +566,7 @@
             pltpu.SemaphoreType.DMA((n_out, n)),
             pltpu.SemaphoreType.DMA((n_out,)),
         ],
-        compiler_params=pltpu.CompilerParams(collective_id=1, has_side_effects=True, vmem_limit_bytes=63 << 20),
+        compiler_params=pltpu.CompilerParams(collective_id=1, has_side_effects=True, vmem_limit_bytes=55 << 20),
         name="tail",
     )(h, mg, wg, wu, wd, ug, wx, cw, cb, wxp_t, dtn, bn, cn, wdt, dtb, alog_t, dsk, wz, wo)
 

time: 175 us -> 170 us (0.971)
  Pallas kernels: 172 us -> 168 us
    pallas_call x1, Pallas kernels: 126 us -> 121 us  [tail(): pl.pallas_call(functools.partial(tail_kernel, n, seq, dt_rank, n_state),...]
where the time goes in v4:
time: 170 us
  Pallas kernels  168 us (99%)
  local copies, waits for them, and re-layouts  2.46 us (1%)
    pallas_call x1, Pallas kernels, tail(): pl.pallas_call(functools.partial(tail_kernel, n, seq, dt_rank, n_state),...  121 us
    pallas_call x1, Pallas kernels, head(): pl.pallas_call(functools.partial(head_kernel, n, heads, kvh, hd), out_sha...  46.1 us

profile of v4, /device:TPU:112, one launch (start us, length us, event | category | flops | bytes accessed | tf_op | source)
XLA Modules:
  0.0 170.0 jit_solution(2480765452685840258)
XLA Ops:
  0.0 46.1 %head.1.h_ref = bf16[256,2560]{1,0:T(8,128)(2,1)} custom-call(bf16[16,16,2560]{2,1,0:T(8,128)(2,1)} %x_hbm.1, bf16[2560]{0:T(1024)(128)(2,1)} %g_ref.1, bf16[81920,128]{1,0:T(8,128)(2,1)} %bitcast.11, bf16[20480,128]{1,0:T(8,128)(2,1)} %bitcast.13, bf16[20480,128]{1,0:T(8,128)(2,1)} %bitcast.14, bf16[4096,2560]{1,0:T(8,128)(2,1)} %bitcast.12), custom_call_target="tpu_custom_call" | custom-call | tf_op jit(solution)/shard_map/head/pallas_call | solution.py:217
  46.1 121.4 %tail.1 = bf16[16,16,2560]{2,1,0:T(8,128)(2,1)} custom-call(bf16[256,2560]{1,0:T(8,128)(2,1)} %head.1.h_ref, bf16[2560]{0:T(1024)(128)(2,1)} %mg_ref.1, bf16[2560,9728]{1,0:T(8,128)(2,1)} %wg_hbm.1, bf16[2560,9728]{1,0:T(8,128)(2,1)} %wu_hbm.1, bf16[9728,2560]{1,0:T(8,128)(2,1)} %wd_hbm.1, bf16[2560]{0:T(1024)(128)(2,1)} %ug_ref.1, ...), custom_call_target="tpu_custom_call" | custom-call | tf_op jit(solution)/shard_map/tail/pallas_call | solution.py:535
  167.6 2.5 %copy.26 = bf16[16,16,2560]{2,1,0:T(8,128)(2,1)} copy(bf16[16,16,2560]{2,1,0:T(8,128)(2,1)} %tail.1) | data formatting | bytes 2621440

commit v5 on v4

--- a/solution.py
+++ b/solution.py
@@ -63,7 +63,7 @@
 
 
 def head_kernel(n, heads, kvh, hd, x_hbm, g_ref, wq_hbm, wk_hbm, wv_hbm, wo_hbm, h_ref,
-                x_s, w_s, qb_s, kvb_s, wo_s, a_s, kv_s, q_s, acc_s, pq_s, pk_s,
+                x_s, w_s, qb_s, kvb_s, wo_s, a_s, kv_s, q_s, o_s, acc_s, pq_s, pk_s,
                 ssem, rsem, lsem, qsem, kvsem, osem):
     me = lax.axis_index("sp")
     nb, seq, dm = x_s.shape
@@ -163,42 +163,53 @@
         for h in range(grp):
             kv_s[c * grp + h] = val[:, h * hd:(h + 1) * hd]
         return 0
-    lax.fori_loop(0, 2 * kvh // grp, kv_proj, 0)
+    lax.fori_loop(0, 2 * kvh // grp, kv_proj, 0, unroll=True)
 
     q_s[0] = dot(a_s[...], w_s[:, 0:tile]).astype(BF16)
+    o_s[1] = jnp.zeros_like(o_s[1])
     row_t = lax.broadcasted_iota(jnp.int32, (grp * seq, seq), 0) % seq
     col_t = lax.broadcasted_iota(jnp.int32, (grp * seq, seq), 1)
     causal = row_t >= col_t
 
     def group(j, _):
-        slot = lax.rem(j, slots_o)
+        done = jnp.maximum(j - 1, 0)
+        slot = lax.rem(done, slots_o)
         nxt = jnp.minimum(j + 1, n_o - 1)
         cur = lax.rem(j, 2)
-        q_next = dot(a_s[...], w_s[:, pl.ds(pl.multiple_of(nxt * tile, tile), tile)]).astype(BF16)
-        outs = []
+
+        @pl.when(j != 1)
+        def _():
+            for cp in o_copies(done, slot):
+                cp.wait()
+
+        scores = []
         for b in range(nb):
             qb = q_s[cur, b * seq:(b + 1) * seq, :]
             q4 = jnp.concatenate([qb[:, g * hd:(g + 1) * hd] for g in range(grp)], axis=0)
-            kb = kv_s[j, b * seq:(b + 1) * seq, :]
-            vb = kv_s[kvh + j, b * seq:(b + 1) * seq, :]
-            s = dot_nt(q4, kb) * (hd ** -0.5)
-            s = jnp.where(causal, s, -jnp.inf)
+            scores.append(dot_nt(q4, kv_s[j, b * seq:(b + 1) * seq, :]))
+        q_next = dot(a_s[...], w_s[:, pl.ds(pl.multiple_of(nxt * tile, tile), tile)]).astype(BF16)
+        probs = []
+        for s in scores:
+            s = jnp.where(causal, s * (hd ** -0.5), -jnp.inf)
             e = jnp.exp(s - jnp.max(s, axis=-1, keepdims=True))
-            p = (e / jnp.sum(e, axis=-1, keepdims=True)).astype(BF16)
-            o = dot(p, vb).astype(BF16)
-            outs.append(jnp.concatenate([o[g * seq:(g + 1) * seq, :] for g in range(grp)], axis=1))
+            probs.append((e / jnp.sum(e, axis=-1, keepdims=True)).astype(BF16))
+        acc_s[...] += dot(o_s[1 - cur], wo_s[slot])
+        for b in range(nb):
+            o = dot(probs[b], kv_s[kvh + j, b * seq:(b + 1) * seq, :]).astype(BF16)
+            for g in range(grp):
+                o_s[cur, b * seq:(b + 1) * seq, g * hd:(g + 1) * hd] = o[g * seq:(g + 1) * seq, :]
         q_s[1 - cur] = q_next
-        for cp in o_copies(j, slot):
-            cp.wait()
-        acc_s[...] += dot(jnp.concatenate(outs, axis=0), wo_s[slot])
-
-        @pl.when(j + slots_o < n_o)
-        def _():
-            for cp in o_copies(j + slots_o, slot):
+
+        @pl.when((j >= 1) & (j - 1 + slots_o < n_o))
+        def _():
+            for cp in o_copies(j - 1 + slots_o, slot):
                 cp.start()
         return 0
     lax.fori_loop(0, n_o, group, 0)
-    h_ref[...] = acc_s[...].astype(BF16)
+    last = (n_o - 1) % slots_o
+    for cp in o_copies(n_o - 1, last):
+        cp.wait()
+    h_ref[...] = (acc_s[...] + dot(o_s[(n_o - 1) % 2], wo_s[last])).astype(BF16)
 
 
 def head(x, g, wq, wk, wv, wo, n):
@@ -227,6 +238,7 @@
             pltpu.VMEM((slots_o, tile, dm), BF16),
             pltpu.VMEM((rows, dm), BF16),
             pltpu.VMEM((2 * kvh, rows, hd), BF16),
+            pltpu.VMEM((2, rows, tile), BF16),
             pltpu.VMEM((2, rows, tile), BF16),
             pltpu.VMEM((rows, dm), F32),
             pltpu.VMEM((blk, blk), BF16),

time: 170 us -> 166 us (0.976)
  Pallas kernels: 168 us -> 163 us
    pallas_call x1, Pallas kernels: 46.1 us -> 41.5 us  [head(): pl.pallas_call(functools.partial(head_kernel, n, heads, kvh, hd), out_sha...]
where the time goes in v5:
time: 166 us; the launch traced here: 165 us
  Pallas kernels  163 us (98%)
  local copies, waits for them, and re-layouts  2.46 us (1%)
    pallas_call x1, Pallas kernels, tail(): pl.pallas_call(functools.partial(tail_kernel, n, seq, dt_rank, n_state),...  121 us
    pallas_call x1, Pallas kernels, head(): pl.pallas_call(functools.partial(head_kernel, n, heads, kvh, hd), out_sha...  41.5 us

profile of v5, /device:TPU:112, one launch (start us, length us, event | category | flops | bytes accessed | tf_op | source)
XLA Modules:
  0.0 165.3 jit_solution(12880271990957455642)
XLA Ops:
  0.0 41.5 %head.1.h_ref = bf16[256,2560]{1,0:T(8,128)(2,1)} custom-call(bf16[16,16,2560]{2,1,0:T(8,128)(2,1)} %x_hbm.1, bf16[2560]{0:T(1024)(128)(2,1)} %g_ref.1, bf16[81920,128]{1,0:T(8,128)(2,1)} %bitcast.11, bf16[20480,128]{1,0:T(8,128)(2,1)} %bitcast.13, bf16[20480,128]{1,0:T(8,128)(2,1)} %bitcast.14, bf16[4096,2560]{1,0:T(8,128)(2,1)} %bitcast.12), custom_call_target="tpu_custom_call" | custom-call | tf_op jit(solution)/shard_map/head/pallas_call | solution.py:228
  41.5 121.3 %tail.1 = bf16[16,16,2560]{2,1,0:T(8,128)(2,1)} custom-call(bf16[256,2560]{1,0:T(8,128)(2,1)} %head.1.h_ref, bf16[2560]{0:T(1024)(128)(2,1)} %mg_ref.1, bf16[2560,9728]{1,0:T(8,128)(2,1)} %wg_hbm.1, bf16[2560,9728]{1,0:T(8,128)(2,1)} %wu_hbm.1, bf16[9728,2560]{1,0:T(8,128)(2,1)} %wd_hbm.1, bf16[2560]{0:T(1024)(128)(2,1)} %ug_ref.1, ...), custom_call_target="tpu_custom_call" | custom-call | tf_op jit(solution)/shard_map/tail/pallas_call | solution.py:547
  162.8 2.5 %copy.26 = bf16[16,16,2560]{2,1,0:T(8,128)(2,1)} copy(bf16[16,16,2560]{2,1,0:T(8,128)(2,1)} %tail.1) | data formatting | bytes 2621440

commit v6 on v5

--- a/solution.py
+++ b/solution.py
@@ -533,7 +533,7 @@
         cp.wait()
 
 
-def tail(h, mg, wg, wu, wd, ug, wx, wz, cw, cb, wxp_t, dtn, bn, cn, wdt, dtb, alog_t, dsk, wo, seq, n, half_w=512, n_out=5, slots=3, slots_d=4):
+def tail(h, mg, wg, wu, wd, ug, wx, wz, cw, cb, wxp_t, dtn, bn, cn, wdt, dtb, alog_t, dsk, wo, seq, n, half_w=512, n_out=10, slots=3, slots_d=4):
     rows, dm = h.shape
     inner = wx.shape[1]
     dt_rank, n_state = wdt.shape[0], alog_t.shape[0]

time: 166 us -> 166 us (level)
  no operation moved by 1% of the time
where the time goes in v6:
time: 166 us
  Pallas kernels  163 us (98%)
  local copies, waits for them, and re-layouts  2.46 us (1%)
    pallas_call x1, Pallas kernels, tail(): pl.pallas_call(functools.partial(tail_kernel, n, seq, dt_rank, n_state),...  122 us
    pallas_call x1, Pallas kernels, head(): pl.pallas_call(functools.partial(head_kernel, n, heads, kvh, hd), out_sha...  41.5 us

profile of v6, /device:TPU:112, one launch (start us, length us, event | category | flops | bytes accessed | tf_op | source)
XLA Modules:
  0.0 165.7 jit_solution(9255256532600197254)
XLA Ops:
  0.0 41.5 %head.1.h_ref = bf16[256,2560]{1,0:T(8,128)(2,1)} custom-call(bf16[16,16,2560]{2,1,0:T(8,128)(2,1)} %x_hbm.1, bf16[2560]{0:T(1024)(128)(2,1)} %g_ref.1, bf16[81920,128]{1,0:T(8,128)(2,1)} %bitcast.11, bf16[20480,128]{1,0:T(8,128)(2,1)} %bitcast.13, bf16[20480,128]{1,0:T(8,128)(2,1)} %bitcast.14, bf16[4096,2560]{1,0:T(8,128)(2,1)} %bitcast.12), custom_call_target="tpu_custom_call" | custom-call | tf_op jit(solution)/shard_map/head/pallas_call | solution.py:228
  41.5 121.7 %tail.1 = bf16[16,16,2560]{2,1,0:T(8,128)(2,1)} custom-call(bf16[256,2560]{1,0:T(8,128)(2,1)} %head.1.h_ref, bf16[2560]{0:T(1024)(128)(2,1)} %mg_ref.1, bf16[2560,9728]{1,0:T(8,128)(2,1)} %wg_hbm.1, bf16[2560,9728]{1,0:T(8,128)(2,1)} %wu_hbm.1, bf16[9728,2560]{1,0:T(8,128)(2,1)} %wd_hbm.1, bf16[2560]{0:T(1024)(128)(2,1)} %ug_ref.1, ...), custom_call_target="tpu_custom_call" | custom-call | tf_op jit(solution)/shard_map/tail/pallas_call | solution.py:547
  163.3 2.5 %copy.26 = bf16[16,16,2560]{2,1,0:T(8,128)(2,1)} copy(bf16[16,16,2560]{2,1,0:T(8,128)(2,1)} %tail.1) | data formatting | bytes 2621440
